TPU v7x, 128 devices: a whole 4x4x4 slice. The times are simulated.
128 devices in a mesh: tp: 4 (over x), dp: 32 (over z, y, core).
Axes of the slice: x: 4, y: 4, z: 4, core: 2. Of those that a mesh axis runs over, the one named last changes fastest.
Arguments:
- hidden: bfloat16 [128, 128, 4096], P('dp')
- positions: int32 [128], replicated
- ln1_gain: bfloat16 [4096], replicated
- ln1_bias: bfloat16 [4096], replicated
- w_q: bfloat16 [4096, 6144], P(None, 'tp')
- w_k: bfloat16 [4096, 1024], P(None, 'tp')
- w_v: bfloat16 [4096, 1024], P(None, 'tp')
- w_o: bfloat16 [6144, 4096], P('tp')
- ln2_gain: bfloat16 [4096], replicated
- ln2_bias: bfloat16 [4096], replicated
- w_up: bfloat16 [4096, 16384], P(None, 'tp')
- w_down: bfloat16 [16384, 4096], P('tp')
Outputs:
- output 1: bfloat16 [128, 128, 4096], P('dp')
- output 2: float32 [16384], P('tp')
- output 3: float32 [48], P('tp')
- output 4: float32 [4096], replicated
All inputs are finite; a program needn't handle non-finite values.
Results may differ from a plain program's by a relative error of at most 0.0101698.
Values sent between devices are 32-bit elements.
A program may use at most 1 GiB of HBM per device.

v0:
```python
import jax
import jax.numpy as jnp
from jax import lax
from jax.sharding import PartitionSpec as P

HEAD_DIM = 128
ROT_DIM = 64
ROPE_BASE = 10000.0
LN_EPS = 1e-5


def layer_norm_1p(in_rows, ln_gain, ln_bias):
    rows_f32 = in_rows.astype(jnp.float32)
    row_mean = jnp.mean(rows_f32, axis=-1, keepdims=True)
    centered = rows_f32 - row_mean
    row_var = jnp.mean(centered * centered, axis=-1, keepdims=True)
    scaled = centered * lax.rsqrt(row_var + LN_EPS)
    return (scaled * (1.0 + ln_gain.astype(jnp.float32)) + ln_bias.astype(jnp.float32)).astype(jnp.bfloat16)


def rope_tables(positions):
    rot_half = ROT_DIM // 2
    inv_freq = ROPE_BASE ** (-2.0 * jnp.arange(rot_half, dtype=jnp.float32) / ROT_DIM)
    pos_angle = positions.astype(jnp.float32)[:, None] * inv_freq[None, :]
    return jnp.cos(pos_angle), jnp.sin(pos_angle)


def apply_rope(heads_in, cos_b, sin_b):
    rot_half = ROT_DIM // 2
    heads_f32 = heads_in.astype(jnp.float32)
    lead_half = heads_f32[..., :rot_half]
    tail_half = heads_f32[..., rot_half:ROT_DIM]
    turned = jnp.concatenate([lead_half * cos_b - tail_half * sin_b, tail_half * cos_b + lead_half * sin_b], axis=-1)
    return jnp.concatenate([turned.astype(jnp.bfloat16), heads_in[..., ROT_DIM:]], axis=-1)


def attention_block(h_in, positions, w_q, w_k, w_v):
    n_batch = h_in.shape[0]
    n_seq = h_in.shape[1]
    kv_heads = w_k.shape[1] // HEAD_DIM
    q_group = w_q.shape[1] // w_k.shape[1]
    cos_t, sin_t = rope_tables(positions)
    q_proj = jnp.einsum("bsd,dn->bsn", h_in, w_q, preferred_element_type=jnp.float32).astype(jnp.bfloat16)
    q_proj = q_proj.reshape(n_batch, n_seq, kv_heads, q_group, HEAD_DIM)
    k_proj = jnp.einsum("bsd,dn->bsn", h_in, w_k, preferred_element_type=jnp.float32).astype(jnp.bfloat16)
    k_proj = k_proj.reshape(n_batch, n_seq, kv_heads, HEAD_DIM)
    v_proj = jnp.einsum("bsd,dn->bsn", h_in, w_v, preferred_element_type=jnp.float32).astype(jnp.bfloat16)
    v_proj = v_proj.reshape(n_batch, n_seq, kv_heads, HEAD_DIM)
    q_proj = apply_rope(q_proj, cos_t[None, :, None, None, :], sin_t[None, :, None, None, :])
    k_proj = apply_rope(k_proj, cos_t[None, :, None, :], sin_t[None, :, None, :])
    scores = jnp.einsum("bqkgd,bskd->bkgqs", q_proj, k_proj, preferred_element_type=jnp.float32) * HEAD_DIM ** -0.5
    causal = jnp.arange(n_seq)[:, None] >= jnp.arange(n_seq)[None, :]
    scores = jnp.where(causal, scores, -1e30)
    attn_prob = jax.nn.softmax(scores, axis=-1).astype(jnp.bfloat16)
    return jnp.einsum("bkgqs,bskd->bqkgd", attn_prob, v_proj, preferred_element_type=jnp.float32).astype(jnp.bfloat16)


def solution(mesh):
    def local_layer(hidden, positions, ln1_gain, ln1_bias, w_q, w_k, w_v, w_o, ln2_gain, ln2_bias, w_up, w_down):
        n_batch = hidden.shape[0]
        n_seq = hidden.shape[1]
        h_in = layer_norm_1p(hidden, ln1_gain, ln1_bias)
        attn_out = attention_block(h_in, positions, w_q, w_k, w_v)
        head_norm = jnp.sqrt(jnp.sum(jnp.square(attn_out.astype(jnp.float32)), axis=-1)).reshape(n_batch, n_seq, -1)
        o_part = jnp.einsum("bsn,nd->bsd", attn_out.reshape(n_batch, n_seq, -1), w_o, preferred_element_type=jnp.float32)
        o_sum = lax.psum(o_part, "tp")
        x_mid = (hidden.astype(jnp.float32) + o_sum).astype(jnp.bfloat16)
        h_mid = layer_norm_1p(x_mid, ln2_gain, ln2_bias)
        mlp_act = jnp.square(jax.nn.relu(jnp.einsum("bsd,df->bsf", h_mid, w_up, preferred_element_type=jnp.float32)))
        mlp_part = jnp.einsum("bsf,fd->bsd", mlp_act.astype(jnp.bfloat16), w_down, preferred_element_type=jnp.float32)
        mlp_sum = lax.psum(mlp_part, "tp")
        out_hidden = (x_mid.astype(jnp.float32) + mlp_sum).astype(jnp.bfloat16)
        neuron_sq = jnp.sum(jnp.square(jnp.mean(mlp_act, axis=1)), axis=0)
        head_sq = jnp.sum(jnp.square(jnp.mean(head_norm, axis=1)), axis=0)
        ln1_sq = jnp.sum(jnp.square(jnp.mean(h_in, axis=1, dtype=jnp.float32)), axis=0)
        ln2_sq = jnp.sum(jnp.square(jnp.mean(h_mid, axis=1, dtype=jnp.float32)), axis=0)
        packed = jnp.concatenate([neuron_sq, head_sq, ln1_sq + ln2_sq])
        score_roots = jnp.sqrt(lax.psum(packed, "dp"))
        ff_local = neuron_sq.shape[0]
        heads_local = head_sq.shape[0]
        f_neuron = score_roots[:ff_local]
        f_head = score_roots[ff_local:ff_local + heads_local]
        f_embed = score_roots[ff_local + heads_local:]
        return out_hidden, f_neuron, f_head, f_embed

    weight_col = P(None, "tp")
    weight_row = P("tp", None)
    return jax.shard_map(
        local_layer,
        mesh=mesh,
        in_specs=(P("dp"), P(), P(), P(), weight_col, weight_col, weight_col, weight_row, P(), P(), weight_col, weight_row),
        out_specs=(P("dp"), P("tp"), P("tp"), P()),
        check_vma=False,
    )
```

profile of v0, /device:TPU:1, one launch (start us, length us, event | category | flops | bytes accessed | tf_op | source)
XLA Modules:
  0.0 573.1 jit_solution(11398661648450730243)
XLA Ops:
  7.3 3.0 convert_reduce_fusion.1
  10.8 1.2 fusion.17
  12.1 11.6 %fusion.27 = bf16[4,128,1536]{2,1,0:T(8,128)(2,1)} fusion(bf16[4096,1536]{1,0:T(8,128)(2,1)} %param.16, bf16[4,128,4096]{2,1,0:T(8,128)(2,1)S(1)} %copy-done.3, f32[4096]{0:T(1024)S(1)} %convert_element_type.75, f32[4096]{0:T(1024)S(1)} %convert_add_fusion.3, f32[4,128]{1,0:T(4,128)S(1)} %add_rsqrt_fusion.1, f32[4,128]{1,0:T(4,128)S(1)} %broadcast_multiply_fusion.1), kind=kOutput, calls=%fused_computation.41 | convolution fusion | flops 6455820288 | bytes 18386944 | tf_op jit(solution)/shard_map/bsd,dn->bsn/dot_general | solution.py:43
  23.7 2.6 copy.58
  26.3 2.6 copy.59
  28.9 3.2 slice.41
  32.1 3.4 convert_element_type.82
  35.6 1.8 fusion.51
  37.4 1.8 fusion.45
  40.1 1.1 copy-done.5
  41.2 1.0 subtract_convert_fusion
  42.6 1.9 fusion.36
  44.5 0.8 fusion.70
  45.3 0.7 multiply_reduce_fusion
  46.1 1.6 slice-done.2
  47.7 9.1 %fusion.5 = f32[4,128,4096]{2,1,0:T(8,128)} fusion(bf16[4,128,1536]{1,2,0:T(8,128)(2,1)S(1)} %bitcast.66, bf16[1536,4096]{1,0:T(8,128)(2,1)S(1)} %bitcast.65), kind=kOutput, calls=%fused_computation.5 | convolution fusion | flops 6442450944 | bytes 22544384 | tf_op jit(solution)/shard_map/bsn,nd->bsd/dot_general | solution.py:65
  57.6 162.3 %all-reduce.3.cloned.1.call-done = f32[4,128,4096]{2,1,0:T(8,128)} async-done(((f32[4,128,4096]{2,1,0:T(8,128)}), f32[4,128,4096]{2,1,0:T(8,128)}) %all-reduce.3.cloned.1.call-update) | async-done | bytes 8388624 | tf_op jit(solution)/shard_map/psum | solution.py:66
  219.9 7.6 %convert_reduce_fusion = (f32[4,128]{1,0:T(4,128)S(1)}, bf16[4,128,4096]{2,1,0:T(8,128)(2,1)S(1)}, f32[4,4096]{1,0:T(4,128)S(1)}) fusion(f32[4,128,4096]{2,1,0:T(8,128)} %all-reduce.3.cloned.1.call-done, bf16[4,128,4096]{2,1,0:T(8,128)(2,1)} %param.12, f32[4096]{0:T(1024)S(1)} %convert_element_type.75, f32[4096]{0:T(1024)S(1)} %convert_add_fusion.3, ...), kind=kLoop, calls=%fused_computation.11 | loop fusion | flops 25148928 | bytes 16881664 | tf_op jit(solution)/shard_map/reduce_sum | solution.py:14
  227.5 1.2 fusion.13
  228.7 22.3 %fusion.23 = (f32[4,4096]{1,0:T(4,128)S(1)}, f32[4,128,4096]{2,1,0:T(8,128)S(1)}) fusion(bf16[4096,4096]{1,0:T(8,128)(2,1)} %param.22, bf16[4,128,4096]{2,1,0:T(8,128)(2,1)S(1)} %get-tuple-element.5, f32[4096]{0:T(1024)S(1)} %convert_element_type.89, f32[4096]{0:T(1024)S(1)} %convert_add_fusion.2, f32[4,128]{1,0:T(4,128)S(1)} %add_rsqrt_fusion, ...), kind=kOutput, calls=%fused_computation.32 | convolution fusion | flops 17198727168 | bytes 46239744 | tf_op jit(solution)/shard_map/bsd,df->bsf/dot_general | solution.py:69
  251.1 23.1 %fusion.1 = f32[4,128,4096]{2,1,0:T(8,128)} fusion(bf16[4096,4096]{1,0:T(8,128)(2,1)} %param.23, f32[4,128,4096]{2,1,0:T(8,128)S(1)} %get-tuple-element.22), kind=kOutput, calls=%fused_computation.1 | convolution fusion | flops 17186160640 | bytes 50331648 | tf_op jit(solution)/shard_map/bsf,fd->bsd/dot_general | solution.py:70
  274.5 159.6 %all-reduce.5.cloned.1.call-done = f32[4,128,4096]{2,1,0:T(8,128)} async-done(((f32[4,128,4096]{2,1,0:T(8,128)}), f32[4,128,4096]{2,1,0:T(8,128)}) %all-reduce.5.cloned.1.call-update) | async-done | bytes 8388624 | tf_op jit(solution)/shard_map/psum | solution.py:71
  434.1 7.4 %convert_reduce_fusion.2 = (f32[4,4096]{1,0:T(4,128)S(1)}, bf16[4,128,4096]{2,1,0:T(8,128)(2,1)}) fusion(f32[4096]{0:T(1024)S(1)} %convert_element_type.89, f32[4096]{0:T(1024)S(1)} %convert_add_fusion.2, f32[4,128]{1,0:T(4,128)S(1)} %add_rsqrt_fusion, f32[4,128]{1,0:T(4,128)S(1)} %broadcast_multiply_fusion, bf16[4,128,4096]{2,1,0:T(8,128)(2,1)} %copy-done.2, ...), kind=kLoop, calls=%fused_computation.29 | loop fusion | flops 20955136 | bytes 16879616 | tf_op jit(solution)/shard_map/reduce_sum | solution.py:76
  441.7 123.3 %psum.23 = f32[8204]{0:T(1024)S(1)} all-reduce(f32[8204]{0:T(1024)S(1)} %concatenate.17), channel_id=1, replica_groups=mesh['tp'=4,'dp'=32] {'dp'}, use_global_device_ids=true, to_apply=%region_17.18 | all-reduce | flops 8204 | bytes 65632 | tf_op jit(solution)/shard_map/psum | solution.py:78
  (61 shorter events, 4.4 us)
Async XLA Ops:
  7.2 28.4 %copy-start = (bf16[4096,256]{1,0:T(8,128)(2,1)S(1)}, bf16[4096,256]{1,0:T(8,128)(2,1)}, u32[]{:S(2)}) copy-start(bf16[4096,256]{1,0:T(8,128)(2,1)} %param.17) | copy-start | bytes 6291460
  7.2 212.7 %all-reduce.3.cloned.1.call-start = ((), (), s32[]{:S(2)}) async-start(), calls=%async_computation | async-start | bytes 16777216 | tf_op jit(solution)/shard_map/psum | solution.py:66
  7.2 3.6 copy-start.3
  7.3 4.8 copy-start.7
  7.3 4.8 copy-start.8
  28.9 6.7 %copy-start.12 = (s32[128]{0:T(128)S(1)}, s32[128]{0:T(128)}, u32[]{:S(2)}) copy-start(s32[128]{0:T(128)} %param.13) | copy-start | bytes 1540
  28.9 6.7 %copy-start.4 = (bf16[4,128,4096]{2,1,0:T(8,128)(2,1)S(1)}, bf16[4,128,4096]{2,1,0:T(8,128)(2,1)}, u32[]{:S(2)}) copy-start(bf16[4,128,4096]{2,1,0:T(8,128)(2,1)} %param.12) | copy-start | bytes 12582916
  35.6 1.8 copy-start.11
  39.3 1.9 copy-start.5
  41.2 1.4 copy-start.6
  42.6 3.4 slice-start
  42.6 3.5 slice-start.1
  45.3 2.4 slice-start.2
  56.8 0.7 copy-start.9
  56.8 0.7 copy-start.10
  56.9 377.2 %all-reduce.5.cloned.1.call-start = ((), (), s32[]{:S(2)}) async-start(), calls=%async_computation.1 | async-start | bytes 16777216 | tf_op jit(solution)/shard_map/psum | solution.py:71
  227.5 23.6 %copy-start.2 = (bf16[4,128,4096]{2,1,0:T(8,128)(2,1)}, bf16[4,128,4096]{2,1,0:T(8,128)(2,1)S(1)}, u32[]{:S(2)}) copy-start(bf16[4,128,4096]{2,1,0:T(8,128)(2,1)S(1)} %get-tuple-element.5) | copy-start | bytes 12582916
  434.1 132.2 %copy-start.1 = (bf16[4096,256]{1,0:T(8,128)(2,1)S(1)}, bf16[4096,256]{1,0:T(8,128)(2,1)}, u32[]{:S(2)}) copy-start(bf16[4096,256]{1,0:T(8,128)(2,1)} %param.17) | copy-start | bytes 6291460
Sparse Core Ops, SparseCore 0:
  57.0 162.8 all-reduce.2
  274.3 159.7 all-reduce.4
where the time goes:
time: 578 us; the launch traced here: 573 us
  waiting for transfers between devices  322 us (56%)
  blocking collectives  123 us (21%)
  matrix products  72.2 us (12%)
  other arithmetic  26.7 us (5%)
  local copies, waits for them, and re-layouts  14.4 us (2%)
  between operations  14.3 us (2%)
    psum x1, waiting for transfers between devices, local_layer(): o_sum = lax.psum(o_part, 'tp')  162 us
    psum x1, waiting for transfers between devices, local_layer(): mlp_sum = lax.psum(mlp_part, 'tp')  160 us
    psum x1, blocking collectives, local_layer(): score_roots = jnp.sqrt(lax.psum(packed, 'dp'))  123 us
    dot_general x1, matrix products, local_layer(): jnp.einsum('bsf,fd->bsd', mlp_act.astype(jnp.bfloat16), w_down, preferred...  23.1 us
    dot_general x1, matrix products, local_layer(): jnp.einsum('bsd,df->bsf', h_mid, w_up, preferred_element_type=jnp.float32)  22.3 us
    dot_general x1, matrix products, attention_block(): jnp.einsum('bsd,dn->bsn', h_in, w_q, preferred_element_type=jnp.float32)  11.6 us
  transfers between devices with their start and end apart: 2, of which 2 were waited for; matrix products, arithmetic and copies ran while one was open for 0% of the time, Pallas kernels for 0%

commit v1 on v0

--- a/solution.py
+++ b/solution.py
@@ -1,12 +1,29 @@
+import functools
+
 import jax
 import jax.numpy as jnp
 from jax import lax
+from jax.experimental import pallas as pl
+from jax.experimental.pallas import tpu as pltpu
 from jax.sharding import PartitionSpec as P
 
 HEAD_DIM = 128
 ROT_DIM = 64
 ROPE_BASE = 10000.0
 LN_EPS = 1e-5
+TILE = 512
+NSLOT = 3
+MESH = pl.DeviceIdType.MESH
+
+UNITS = (
+    ("rs1", 0), ("rs1", 1), ("ag1", 0), ("rs1", 2), ("ag1", 1), ("rs1", 3), ("rs2", 0), ("ag1", 2),
+    ("rs2", 1), ("ag1", 3), ("ag2", 0), ("rs2", 2), ("ag2", 1), ("rs2", 3), ("ag2", 2), ("ag2", 3),
+)
+HEAD_PIECES = (("o", 0), ("o", 1))
+SLOT_PIECES = {
+    0: (("o", 2),), 2: (("o", 3),), 3: (("up", 0),), 4: (("dn", 0),), 5: (("up", 1),), 6: (("dn", 1),),
+    8: (("up", 2),), 9: (("dn", 2),), 10: (("up", 3),), 11: (("dn", 3),),
+}
 
 
 def layer_norm_1p(in_rows, ln_gain, ln_bias):
@@ -55,33 +72,324 @@
     return jnp.einsum("bkgqs,bskd->bqkgd", attn_prob, v_proj, preferred_element_type=jnp.float32).astype(jnp.bfloat16)
 
 
+def layer_kernel(
+    n_tp, n_dp, attn_ref, esq_ref, head_ref, gain_ref, bias_ref, hid_ref, wo_ref, wup_ref, wdn_ref,
+    y_ref, score_ref,
+    wbuf, part, rbuf, gath, hmid, act, xmid, ystage, nsq, esq, sbuf, xbuf,
+    wsem, ssem, rsem, hsem, ysem, xssem, xrsem,
+):
+    me = lax.axis_index("tp")
+    my_dp = lax.axis_index("dp")
+    right = lax.rem(me + 1, n_tp)
+    left = lax.rem(me + n_tp - 1, n_tp)
+    opp = lax.rem(me + 2, n_tp)
+    n_seq = part.shape[1]
+    width = part.shape[2]
+    blk = n_seq // n_tp
+    half = blk // 2
+    k_o = wo_ref.shape[0]
+    partners = []
+    step = 1
+    while step < n_dp:
+        bit = lax.rem(my_dp // step, 2)
+        partners.append(my_dp + step - 2 * step * bit)
+        step *= 2
+
+    def half_rows(owner, which):
+        return pl.ds(pl.multiple_of(owner * blk + which * half, half), half)
+
+    pieces = list(HEAD_PIECES)
+    for k in range(len(UNITS)):
+        pieces.extend(SLOT_PIECES.get(k, ()))
+
+    def n_tiles(kind):
+        return (wup_ref if kind == "up" else wdn_ref).shape[1] // TILE
+
+    bases = {}
+    base = 0
+    for piece in pieces:
+        bases[piece] = base
+        base += n_tiles(piece[0])
+
+    def tile_copy(piece, i):
+        slot = lax.rem(bases[piece] + i, NSLOT)
+        cols = pl.ds(pl.multiple_of(i * TILE, TILE), TILE)
+        if piece[0] == "o":
+            return pltpu.make_async_copy(wo_ref.at[:, cols], wbuf.at[slot, pl.ds(0, k_o), :], wsem.at[slot])
+        src = wup_ref if piece[0] == "up" else wdn_ref
+        return pltpu.make_async_copy(src.at[:, cols], wbuf.at[slot], wsem.at[slot])
+
+    def prefetch(piece):
+        for i in range(NSLOT - 1):
+            tile_copy(piece, i).start()
+
+    def run_piece(piece):
+        kind, seq = piece
+        tiles = n_tiles(kind)
+
+        def body(i, carry):
+            tile_copy(piece, i).wait()
+
+            @pl.when(i + NSLOT - 1 < tiles)
+            def _():
+                tile_copy(piece, i + NSLOT - 1).start()
+
+            slot = lax.rem(bases[piece] + i, NSLOT)
+            cols = pl.ds(pl.multiple_of(i * TILE, TILE), TILE)
+            if kind == "o":
+                part[seq % 3, :, cols] = jnp.dot(
+                    attn_ref[seq], wbuf[slot, pl.ds(0, k_o), :], preferred_element_type=jnp.float32
+                )
+            elif kind == "up":
+                up = jnp.maximum(jnp.dot(hmid[...], wbuf[slot], preferred_element_type=jnp.float32), 0.0)
+                sq = up * up
+                mean = jnp.sum(sq, axis=0, keepdims=True) * (1.0 / n_seq)
+                nsq[:, cols] += mean * mean
+                act[:, cols] = sq.astype(jnp.bfloat16)
+            else:
+                part[(4 + seq) % 3, :, cols] = jnp.dot(act[...], wbuf[slot], preferred_element_type=jnp.float32)
+            return carry
+
+        lax.fori_loop(0, tiles, body, 0)
+        after = pieces.index(piece) + 1
+        if after < len(pieces):
+            prefetch(pieces[after])
+
+    def remote(src, dst, k, direction, j):
+        return pltpu.make_async_remote_copy(
+            src_ref=src, dst_ref=dst, send_sem=ssem.at[k, direction, j], recv_sem=rsem.at[k, direction, j],
+            device_id={"tp": right if direction == 0 else left}, device_id_type=MESH,
+        )
+
+    def unit_copies(k):
+        kind, seq = UNITS[k]
+        ix = seq if kind[2] == "1" else 4 + seq
+        if kind[:2] == "rs":
+            p = ix % 3
+            routes = (
+                ((opp, 0), (right, 1), (right, 0)),
+                ((opp, 1), (left, 0), (left, 1)),
+            )
+            return [
+                [
+                    remote(part.at[p, half_rows(*routes[d][j]), :], rbuf.at[ix, d, j], k, d, j)
+                    for j in range(3)
+                ]
+                for d in range(2)
+            ]
+        routes = (
+            ((me, 0), (me, 1), (left, 0)),
+            ((me, 1), (me, 0), (right, 1)),
+        )
+        return [
+            [
+                remote(
+                    gath.at[ix, half_rows(*routes[d][j]), :], gath.at[ix, half_rows(*routes[d][j]), :], k, d, j
+                )
+                for j in range(3)
+            ]
+            for d in range(2)
+        ]
+
+    copies = [unit_copies(k) for k in range(len(UNITS))]
+
+    def begin(k):
+        for j in range(2):
+            for d in range(2):
+                copies[k][d][j].start()
+
+    def middle(k):
+        kind, seq = UNITS[k]
+        ix = seq if kind[2] == "1" else 4 + seq
+        for d in range(2):
+            copies[k][d][0].wait_recv()
+            if kind[:2] == "rs":
+                rows = half_rows(right if d == 0 else left, d)
+                part[ix % 3, rows, :] = part[ix % 3, rows, :] + rbuf[ix, d, 0]
+            copies[k][d][2].start()
+
+    def norm_rows(rows):
+        mean = jnp.sum(rows, axis=-1, keepdims=True) * (1.0 / width)
+        centered = rows - mean
+        var = jnp.sum(centered * centered, axis=-1, keepdims=True) * (1.0 / width)
+        scaled = centered * lax.rsqrt(var + LN_EPS)
+        out = scaled * (1.0 + gain_ref[...].astype(jnp.float32)) + bias_ref[...].astype(jnp.float32)
+        return out.astype(jnp.bfloat16).astype(jnp.float32)
+
+    def finish(k):
+        kind, seq = UNITS[k]
+        ix = seq if kind[2] == "1" else 4 + seq
+        for d in range(2):
+            for j in (1, 2):
+                copies[k][d][j].wait_recv()
+        if kind[:2] == "rs":
+            for w in range(2):
+                rows = half_rows(me, w)
+                total = part[ix % 3, rows, :] + rbuf[ix, w, 2] + rbuf[ix, 1 - w, 1]
+                mine = pl.ds(w * half, half)
+                mid = (xmid[seq, mine, :].astype(jnp.float32) + total).astype(jnp.bfloat16)
+                if kind == "rs1":
+                    xmid[seq, mine, :] = mid
+                    gath[ix, rows, :] = norm_rows(mid.astype(jnp.float32))
+                else:
+                    gath[ix, rows, :] = mid.astype(jnp.float32)
+        elif kind == "ag1":
+            def cast(i, carry):
+                cols = pl.ds(pl.multiple_of(i * TILE, TILE), TILE)
+                got = gath[ix, :, cols]
+                mean = jnp.sum(got, axis=0, keepdims=True) * (1.0 / n_seq)
+                esq[:, cols] += mean * mean
+                hmid[:, cols] = got.astype(jnp.bfloat16)
+                return carry
+
+            lax.fori_loop(0, width // TILE, cast, 0)
+        else:
+            if seq >= 2:
+                y_copy(seq - 2).wait()
+
+            def store(i, carry):
+                cols = pl.ds(pl.multiple_of(i * TILE, TILE), TILE)
+                ystage[seq % 2, :, cols] = gath[ix, :, cols].astype(jnp.bfloat16)
+                return carry
+
+            lax.fori_loop(0, width // TILE, store, 0)
+            y_copy(seq).start()
+        for d in range(2):
+            for j in range(3):
+                copies[k][d][j].wait_send()
+
+    def y_copy(seq):
+        return pltpu.make_async_copy(ystage.at[seq % 2], y_ref.at[seq], ysem.at[seq % 2])
+
+    def score_copy(i):
+        return pltpu.make_async_remote_copy(
+            src_ref=sbuf.at[i], dst_ref=xbuf.at[i], send_sem=xssem.at[i], recv_sem=xrsem.at[i],
+            device_id={"dp": partners[i]}, device_id_type=MESH,
+        )
+
+    def score_begin():
+        per = width // 8
+        fper = nsq.shape[1] // 8
+        for r in range(8):
+            sbuf[0, r : r + 1, 0:fper] = nsq[:, r * fper : (r + 1) * fper]
+            sbuf[0, r : r + 1, fper : fper + per] = esq[:, r * per : (r + 1) * per]
+            sbuf[0, r : r + 1, fper + per : fper + per + 128] = head_ref[...]
+        score_copy(0).start()
+
+    def score_step(i):
+        score_copy(i).wait()
+        sbuf[i + 1] = sbuf[i] + xbuf[i]
+        if i + 1 < len(partners):
+            score_copy(i + 1).start()
+
+    prefetch(pieces[0])
+    hid_copies = [
+        pltpu.make_async_copy(
+            hid_ref.at[seq, pl.ds(pl.multiple_of(me * blk, blk), blk), :], xmid.at[seq], hsem.at[seq]
+        )
+        for seq in range(hid_ref.shape[0])
+    ]
+    for copy in hid_copies:
+        copy.start()
+    nsq[...] = jnp.zeros_like(nsq)
+    esq[...] = esq_ref[...]
+
+    barrier = pltpu.get_barrier_semaphore()
+    for t in (left, right):
+        pl.semaphore_signal(barrier, inc=1, device_id={"tp": t}, device_id_type=MESH)
+    for other in partners:
+        pl.semaphore_signal(barrier, inc=1, device_id={"dp": other}, device_id_type=MESH)
+    pl.semaphore_wait(barrier, 2 + len(partners))
+
+    run_piece(HEAD_PIECES[0])
+    begin(0)
+    for copy in hid_copies:
+        copy.wait()
+    for piece in HEAD_PIECES[1:]:
+        run_piece(piece)
+    last = len(UNITS) - 1
+    for k in range(len(UNITS)):
+        if k > 0:
+            finish(k - 1)
+        if k < last:
+            begin(k + 1)
+        middle(k)
+        for piece in SLOT_PIECES.get(k, ()):
+            run_piece(piece)
+        if k == 10:
+            score_begin()
+        elif k > 10:
+            score_step(k - 11)
+    finish(last)
+    for i in range(last - 10, len(partners)):
+        score_step(i)
+    score_ref[...] = sbuf[len(partners)]
+    for seq in (2, 3):
+        y_copy(seq).wait()
+
+
 def solution(mesh):
+    n_tp = mesh.shape["tp"]
+    n_dp = mesh.shape["dp"]
+
     def local_layer(hidden, positions, ln1_gain, ln1_bias, w_q, w_k, w_v, w_o, ln2_gain, ln2_bias, w_up, w_down):
-        n_batch = hidden.shape[0]
-        n_seq = hidden.shape[1]
+        n_batch, n_seq, width = hidden.shape
+        ff_local = w_up.shape[1]
         h_in = layer_norm_1p(hidden, ln1_gain, ln1_bias)
         attn_out = attention_block(h_in, positions, w_q, w_k, w_v)
         head_norm = jnp.sqrt(jnp.sum(jnp.square(attn_out.astype(jnp.float32)), axis=-1)).reshape(n_batch, n_seq, -1)
-        o_part = jnp.einsum("bsn,nd->bsd", attn_out.reshape(n_batch, n_seq, -1), w_o, preferred_element_type=jnp.float32)
-        o_sum = lax.psum(o_part, "tp")
-        x_mid = (hidden.astype(jnp.float32) + o_sum).astype(jnp.bfloat16)
-        h_mid = layer_norm_1p(x_mid, ln2_gain, ln2_bias)
-        mlp_act = jnp.square(jax.nn.relu(jnp.einsum("bsd,df->bsf", h_mid, w_up, preferred_element_type=jnp.float32)))
-        mlp_part = jnp.einsum("bsf,fd->bsd", mlp_act.astype(jnp.bfloat16), w_down, preferred_element_type=jnp.float32)
-        mlp_sum = lax.psum(mlp_part, "tp")
-        out_hidden = (x_mid.astype(jnp.float32) + mlp_sum).astype(jnp.bfloat16)
-        neuron_sq = jnp.sum(jnp.square(jnp.mean(mlp_act, axis=1)), axis=0)
         head_sq = jnp.sum(jnp.square(jnp.mean(head_norm, axis=1)), axis=0)
+        heads_local = head_sq.shape[0]
         ln1_sq = jnp.sum(jnp.square(jnp.mean(h_in, axis=1, dtype=jnp.float32)), axis=0)
-        ln2_sq = jnp.sum(jnp.square(jnp.mean(h_mid, axis=1, dtype=jnp.float32)), axis=0)
-        packed = jnp.concatenate([neuron_sq, head_sq, ln1_sq + ln2_sq])
-        score_roots = jnp.sqrt(lax.psum(packed, "dp"))
-        ff_local = neuron_sq.shape[0]
-        heads_local = head_sq.shape[0]
-        f_neuron = score_roots[:ff_local]
-        f_head = score_roots[ff_local:ff_local + heads_local]
-        f_embed = score_roots[ff_local + heads_local:]
-        return out_hidden, f_neuron, f_head, f_embed
+        head_row = jnp.pad(head_sq, (0, 128 - heads_local)).reshape(1, 128)
+        score_cols = ff_local // 8 + width // 8 + 128
+        n_stage = n_dp.bit_length() - 1
+        blk = n_seq // n_tp
+        any_spec = pl.BlockSpec(memory_space=pl.ANY)
+        vmem_spec = pl.BlockSpec(memory_space=pltpu.VMEM)
+        n_units = len(UNITS)
+        y, score = pl.pallas_call(
+            functools.partial(layer_kernel, n_tp, n_dp),
+            out_shape=(
+                jax.ShapeDtypeStruct(hidden.shape, jnp.bfloat16),
+                jax.ShapeDtypeStruct((8, score_cols), jnp.float32),
+            ),
+            in_specs=[vmem_spec] * 5 + [any_spec] * 4,
+            out_specs=(any_spec, vmem_spec),
+            scratch_shapes=[
+                pltpu.VMEM((NSLOT, width, TILE), jnp.bfloat16),
+                pltpu.VMEM((3, n_seq, width), jnp.float32),
+                pltpu.VMEM((2 * n_batch, 2, 3, blk // 2, width), jnp.float32),
+                pltpu.VMEM((2 * n_batch, n_seq, width), jnp.float32),
+                pltpu.VMEM((n_seq, width), jnp.bfloat16),
+                pltpu.VMEM((n_seq, ff_local), jnp.bfloat16),
+                pltpu.VMEM((n_batch, blk, width), jnp.bfloat16),
+                pltpu.VMEM((2, n_seq, width), jnp.bfloat16),
+                pltpu.VMEM((1, ff_local), jnp.float32),
+                pltpu.VMEM((1, width), jnp.float32),
+                pltpu.VMEM((n_stage + 1, 8, score_cols), jnp.float32),
+                pltpu.VMEM((n_stage, 8, score_cols), jnp.float32),
+                pltpu.SemaphoreType.DMA((NSLOT,)),
+                pltpu.SemaphoreType.DMA((n_units, 2, 3)),
+                pltpu.SemaphoreType.DMA((n_units, 2, 3)),
+                pltpu.SemaphoreType.DMA((n_batch,)),
+                pltpu.SemaphoreType.DMA((2,)),
+                pltpu.SemaphoreType.DMA((n_stage,)),
+                pltpu.SemaphoreType.DMA((n_stage,)),
+            ],
+            compiler_params=pltpu.CompilerParams(
+                collective_id=0, has_side_effects=True, vmem_limit_bytes=66_000_000
+            ),
+            name="layer",
+        )(
+            attn_out.reshape(n_batch, n_seq, -1), ln1_sq.reshape(1, width), head_row,
+            ln2_gain.reshape(1, width), ln2_bias.reshape(1, width), hidden, w_o, w_up, w_down,
+        )
+        roots = jnp.sqrt(score)
+        f_neuron = roots[:, : ff_local // 8].reshape(ff_local)
+        f_embed = roots[:, ff_local // 8 : ff_local // 8 + width // 8].reshape(width)
+        f_head = roots[0, ff_local // 8 + width // 8 :][:heads_local]
+        return y, f_neuron, f_head, f_embed
 
     weight_col = P(None, "tp")
     weight_row = P("tp", None)

time: 578 us -> 346 us (0.60)
  the two profiles are of different devices: /device:TPU:1 before, /device:TPU:32 now
where the time goes in v1:
time: 346 us; the launch traced here: 345 us
  Pallas kernels  296 us (86%)
  matrix products  18.7 us (5%)
  local copies, waits for them, and re-layouts  15.9 us (5%)
  other arithmetic  13.4 us (4%)
    pallas_call x1, Pallas kernels, local_layer(): pl.pallas_call(functools.partial(layer_kernel, n_tp, n_dp), out_shape=(ja...  296 us
    dot_general x1, matrix products, attention_block(): jnp.einsum('bsd,dn->bsn', h_in, w_q, preferred_element_type=jnp.float32)  10.7 us
    unnamed x22, local copies, waits for them, and re-layouts  8.38 us

profile of v1, /device:TPU:32, one launch (start us, length us, event | category | flops | bytes accessed | tf_op | source)
XLA Modules:
  0.0 345.1 jit_solution(18208244086946706783)
XLA Ops:
  0.6 3.0 convert_reduce_fusion
  4.1 1.2 fusion.5
  5.4 10.7 %fusion.9 = bf16[4,128,1536]{2,1,0:T(8,128)(2,1)S(1)} fusion(bf16[4096,1536]{1,0:T(8,128)(2,1)} %param.16, bf16[4,128,4096]{2,1,0:T(8,128)(2,1)S(1)} %copy-done, f32[4096]{0:T(1024)S(1)} %convert_element_type.51, f32[4096]{0:T(1024)S(1)} %convert_add_fusion, f32[4,128]{1,0:T(4,128)S(1)} %add_rsqrt_fusion, f32[4,128]{1,0:T(4,128)S(1)} %broadcast_multiply_fusion), kind=kOutput, calls=%fused_computation.18 | convolution fusion | flops 6455820288 | bytes 18386944 | tf_op jit(solution)/shard_map/bsd,dn->bsn/dot_general | solution.py:60
  16.1 0.9 copy.58
  17.0 1.1 copy.59
  19.1 1.1 subtract_convert_fusion
  20.2 1.0 copy-done.1
  21.3 0.7 copy-done.6
  21.9 1.7 fusion.32
  24.1 0.5 slice.47
  24.7 1.9 fusion.17
  26.6 2.4 fusion.48
  29.1 1.8 fusion.26
  31.0 2.6 multiply_reduce_fusion
  33.6 1.6 copy.64.attn_ref
  35.9 3.7 %convert_reduce_fusion.1 = f32[4,4096]{1,0:T(4,128)S(1)} fusion(f32[4096]{0:T(1024)S(1)} %convert_element_type.51, f32[4096]{0:T(1024)S(1)} %convert_add_fusion, f32[4,128]{1,0:T(4,128)S(1)} %add_rsqrt_fusion, f32[4,128]{1,0:T(4,128)S(1)} %broadcast_multiply_fusion, bf16[4,128,4096]{2,1,0:T(8,128)(2,1)} %hid_ref.1), kind=kLoop, calls=%fused_computation.11 | loop fusion | flops 16760832 | bytes 4296704 | tf_op jit(solution)/shard_map/reduce_sum | solution.py:343
  39.7 0.7 multiply_reduce_fusion.1
  40.3 0.6 reshape.170.gain_ref
  41.0 0.6 reshape.171.bias_ref
  41.6 296.3 %layer.1 = (bf16[4,128,4096]{2,1,0:T(8,128)(2,1)}, f32[8,1152]{1,0:T(8,128)}) custom-call(bf16[4,128,1536]{2,1,0:T(8,128)(2,1)} %copy.64.attn_ref, f32[1,4096]{1,0:T(1,128)} %bitcast.64, f32[1,128]{1,0:T(1,128)} %pad_bitcast_fusion.head_ref, bf16[1,4096]{1,0:T(2,128)(2,1)} %reshape.170.gain_ref, bf16[1,4096]{1,0:T(2,128)(2,1)} %reshape.171.bias_ref, ...), custom_call_target="tpu_custom_call" | custom-call | tf_op jit(solution)/shard_map/layer/pallas_call | solution.py:351
  337.9 0.8 sqrt.9
  338.7 0.6 copy.70
  339.3 0.6 copy.71
  340.4 4.7 %copy.81 = bf16[4,128,4096]{2,1,0:T(8,128)(2,1)} copy(bf16[4,128,4096]{2,1,0:T(8,128)(2,1)} %get-tuple-element.26) | data formatting | bytes 8388608
  (35 shorter events, 3.4 us)
Async XLA Ops:
  0.6 3.5 %copy-start = (bf16[4,128,4096]{2,1,0:T(8,128)(2,1)S(1)}, bf16[4,128,4096]{2,1,0:T(8,128)(2,1)}, u32[]{:S(2)}) copy-start(bf16[4,128,4096]{2,1,0:T(8,128)(2,1)} %hid_ref.1) | copy-start | bytes 12582916
  3.6 1.7 copy-start.2
  3.6 1.7 copy-start.3
  18.1 0.7 copy-start.8
  19.1 2.2 copy-start.1
  19.1 2.9 copy-start.6
  26.6 2.5 copy-start.7
  33.6 6.7 %copy-start.4 = (bf16[4096]{0:T(1024)(128)(2,1)S(1)}, bf16[4096]{0:T(1024)(128)(2,1)}, u32[]{:S(2)}) copy-start(bf16[4096]{0:T(1024)(128)(2,1)} %param.20) | copy-start | bytes 24580
  33.6 7.3 %copy-start.5 = (bf16[4096]{0:T(1024)(128)(2,1)S(1)}, bf16[4096]{0:T(1024)(128)(2,1)}, u32[]{:S(2)}) copy-start(bf16[4096]{0:T(1024)(128)(2,1)} %param.21) | copy-start | bytes 24580

commit v2 on v1

v2 whole, which is shorter than its diff:
```python
import functools

import jax
import jax.numpy as jnp
from jax import lax
from jax.experimental import pallas as pl
from jax.experimental.pallas import tpu as pltpu
from jax.sharding import PartitionSpec as P

HEAD_DIM = 128
ROT_DIM = 64
ROPE_BASE = 10000.0
LN_EPS = 1e-5
TILE = 512
NSLOT = 3
MESH = pl.DeviceIdType.MESH

UNITS = (
    ("rs1", 0), ("rs1", 1), ("ag1", 0), ("rs1", 2), ("ag1", 1), ("rs1", 3), ("rs2", 0), ("ag1", 2),
    ("rs2", 1), ("ag1", 3), ("ag2", 0), ("rs2", 2), ("ag2", 1), ("rs2", 3), ("ag2", 2), ("ag2", 3),
)
HEAD_PIECES = (("qkv", 0), ("o", 0), ("qkv", 1), ("o", 1))
SLOT_PIECES = {
    0: (("qkv", 2), ("o", 2)), 2: (("qkv", 3), ("o", 3)), 3: (("up", 0),), 4: (("dn", 0),), 5: (("up", 1),), 6: (("dn", 1),),
    8: (("up", 2),), 9: (("dn", 2),), 10: (("up", 3),), 11: (("dn", 3),),
}


def rope_lanes(positions):
    half_rot = ROT_DIM // 2
    lane = jnp.arange(HEAD_DIM)
    inv_freq = ROPE_BASE ** (-2.0 * (lane % half_rot).astype(jnp.float32) / ROT_DIM)
    angle = positions.astype(jnp.float32)[:, None] * inv_freq[None, :]
    sign = jnp.where(lane < half_rot, -1.0, 1.0)
    cos_l = jnp.where(lane < ROT_DIM, jnp.cos(angle), 1.0)
    sin_l = jnp.where(lane < ROT_DIM, sign * jnp.sin(angle), 0.0)
    return cos_l, sin_l


def layer_kernel(
    n_tp, n_dp, cos_ref, sin_ref, norm_ref, hid_ref, wq_ref, wk_ref, wv_ref, wo_ref, wup_ref, wdn_ref,
    y_ref, score_ref,
    wbuf, part, rbuf, gath, hmid, act, xmid, ystage, nsq, esq, hsq, sbuf, xbuf,
    wsem, vsem, ssem, rsem, hsem, xsem, ysem, xssem, xrsem,
):
    me = lax.axis_index("tp")
    my_dp = lax.axis_index("dp")
    right = lax.rem(me + 1, n_tp)
    left = lax.rem(me + n_tp - 1, n_tp)
    opp = lax.rem(me + 2, n_tp)
    n_seq = part.shape[1]
    width = part.shape[2]
    blk = n_seq // n_tp
    half = blk // 2
    k_o = wo_ref.shape[0]
    partners = []
    step = 1
    while step < n_dp:
        bit = lax.rem(my_dp // step, 2)
        partners.append(my_dp + step - 2 * step * bit)
        step *= 2

    def half_rows(owner, which):
        return pl.ds(pl.multiple_of(owner * blk + which * half, half), half)

    pieces = list(HEAD_PIECES)
    for k in range(len(UNITS)):
        pieces.extend(SLOT_PIECES.get(k, ()))

    n_q = wq_ref.shape[1]
    n_kv = wk_ref.shape[1]
    n_qkv = n_q + 2 * n_kv
    q_tiles = n_q // TILE
    group = n_q // n_kv

    def n_tiles(kind):
        if kind == "qkv":
            return q_tiles + 1
        return (wup_ref if kind == "up" else wdn_ref).shape[1] // TILE

    bases = {}
    base = 0
    for piece in pieces:
        bases[piece] = base
        base += n_tiles(piece[0])

    def tile_slot(piece, i):
        return lax.rem(bases[piece] + i, NSLOT)

    def tile_copy(piece, i):
        slot = tile_slot(piece, i)
        cols = pl.ds(pl.multiple_of(i * TILE, TILE), TILE)
        if piece[0] == "o":
            return pltpu.make_async_copy(wo_ref.at[:, cols], wbuf.at[slot, pl.ds(0, k_o), :], wsem.at[slot])
        src = {"qkv": wq_ref, "up": wup_ref, "dn": wdn_ref}[piece[0]]
        return pltpu.make_async_copy(src.at[:, cols], wbuf.at[slot], wsem.at[slot])

    def kv_copies(piece):
        slot = tile_slot(piece, q_tiles)
        return (
            pltpu.make_async_copy(wk_ref, wbuf.at[slot, :, pl.ds(0, n_kv)], wsem.at[slot]),
            pltpu.make_async_copy(wv_ref, wbuf.at[slot, :, pl.ds(n_kv, n_kv)], vsem),
        )

    def start_tile(piece, i):
        if piece[0] != "qkv":
            tile_copy(piece, i).start()
            return

        @pl.when(i < q_tiles)
        def _():
            tile_copy(piece, i).start()

        @pl.when(i == q_tiles)
        def _():
            for copy in kv_copies(piece):
                copy.start()

    def prefetch(piece):
        for i in range(NSLOT - 1):
            tile_copy(piece, i).start()

    def norm_rows(rows, which):
        mean = jnp.sum(rows, axis=-1, keepdims=True) * (1.0 / width)
        centered = rows - mean
        var = jnp.sum(centered * centered, axis=-1, keepdims=True) * (1.0 / width)
        scaled = centered * lax.rsqrt(var + LN_EPS)
        out = scaled * norm_ref[pl.ds(2 * which, 1), :] + norm_ref[pl.ds(2 * which + 1, 1), :]
        return out.astype(jnp.bfloat16)

    def seq_copy(seq):
        return pltpu.make_async_copy(hid_ref.at[seq], ystage.at[seq % 2], xsem.at[seq % 2])

    def first_norm(seq):
        seq_copy(seq).wait()

        def rows_body(i, carry):
            rows = pl.ds(pl.multiple_of(i * 16, 16), 16)
            hmid[rows, :] = norm_rows(ystage[seq % 2, rows, :].astype(jnp.float32), 0)
            return carry

        lax.fori_loop(0, n_seq // 16, rows_body, 0)
        if seq + 2 < hid_ref.shape[0]:
            seq_copy(seq + 2).start()

    def first_means():
        def cols_body(i, carry):
            cols = pl.ds(pl.multiple_of(i * TILE, TILE), TILE)
            mean = jnp.sum(hmid[:, cols].astype(jnp.float32), axis=0, keepdims=True) * (1.0 / n_seq)
            esq[:, cols] += mean * mean
            return carry

        lax.fori_loop(0, width // TILE, cols_body, 0)

    def rotate(raw, lane):
        rot_half = ROT_DIM // 2
        val = raw.astype(jnp.float32)
        ahead = pltpu.roll(val, HEAD_DIM - rot_half, 1)
        behind = pltpu.roll(val, rot_half, 1)
        partner = jnp.where(lane < rot_half, ahead, behind)
        return (val * cos_ref[...] + partner * sin_ref[...]).astype(jnp.bfloat16)

    def attend():
        lane = lax.broadcasted_iota(jnp.int32, (n_seq, HEAD_DIM), 1)
        row = lax.broadcasted_iota(jnp.int32, (n_seq, n_seq), 0)
        col = lax.broadcasted_iota(jnp.int32, (n_seq, n_seq), 1)
        lane_row = lax.broadcasted_iota(jnp.int32, (1, HEAD_DIM), 1)

        def group_body(g, carry):
            def head_cols(start):
                return pl.ds(pl.multiple_of(start, HEAD_DIM), HEAD_DIM)

            keys = rotate(act[:, head_cols(n_q + g * HEAD_DIM)], lane)
            vals = act[:, head_cols(n_q + n_kv + g * HEAD_DIM)]
            for i in range(group):
                head = g * group + i
                query = rotate(act[:, head_cols(head * HEAD_DIM)], lane)
                scores = lax.dot_general(
                    query, keys, (((1,), (1,)), ((), ())), preferred_element_type=jnp.float32
                ) * HEAD_DIM ** -0.5
                scores = jnp.where(row >= col, scores, -1e30)
                top = jnp.max(scores, axis=-1, keepdims=True)
                exps = jnp.exp(scores - top)
                prob = (exps * (1.0 / jnp.sum(exps, axis=-1, keepdims=True))).astype(jnp.bfloat16)
                out = jnp.dot(prob, vals, preferred_element_type=jnp.float32).astype(jnp.bfloat16)
                act[:, head_cols(n_qkv + head * HEAD_DIM)] = out
                out32 = out.astype(jnp.float32)
                norm = jnp.sqrt(jnp.sum(out32 * out32, axis=-1, keepdims=True))
                mean = jnp.sum(norm, axis=0, keepdims=True) * (1.0 / n_seq)
                hsq[...] += jnp.where(lane_row == head, mean * mean, 0.0)
            return carry

        lax.fori_loop(0, n_kv // HEAD_DIM, group_body, 0)

    def run_piece(piece):
        kind, seq = piece
        tiles = n_tiles(kind)
        if kind == "qkv":
            first_norm(seq)

        def body(i, carry):
            tile_copy(piece, i).wait()

            @pl.when(i + NSLOT - 1 < tiles)
            def _():
                start_tile(piece, i + NSLOT - 1)

            slot = tile_slot(piece, i)
            cols = pl.ds(pl.multiple_of(i * TILE, TILE), TILE)
            if kind == "qkv":
                act[:, cols] = jnp.dot(hmid[...], wbuf[slot], preferred_element_type=jnp.float32).astype(jnp.bfloat16)
            elif kind == "o":
                part[seq % 3, :, cols] = jnp.dot(
                    act[:, pl.ds(n_qkv, n_q)], wbuf[slot, pl.ds(0, k_o), :], preferred_element_type=jnp.float32
                )
            elif kind == "up":
                up = jnp.maximum(jnp.dot(hmid[...], wbuf[slot], preferred_element_type=jnp.float32), 0.0)
                sq = up * up
                mean = jnp.sum(sq, axis=0, keepdims=True) * (1.0 / n_seq)
                nsq[:, cols] += mean * mean
                act[:, cols] = sq.astype(jnp.bfloat16)
            else:
                part[(4 + seq) % 3, :, cols] = jnp.dot(act[...], wbuf[slot], preferred_element_type=jnp.float32)
            return carry

        lax.fori_loop(0, q_tiles if kind == "qkv" else tiles, body, 0)
        if kind == "qkv":
            for copy in kv_copies(piece):
                copy.wait()
            act[:, pl.ds(n_q, 2 * n_kv)] = jnp.dot(
                hmid[...], wbuf[tile_slot(piece, q_tiles)], preferred_element_type=jnp.float32
            ).astype(jnp.bfloat16)
        after = pieces.index(piece) + 1
        if after < len(pieces):
            prefetch(pieces[after])
        if kind == "qkv":
            attend()

    def remote(src, dst, k, direction, j):
        return pltpu.make_async_remote_copy(
            src_ref=src, dst_ref=dst, send_sem=ssem.at[k, direction, j], recv_sem=rsem.at[k, direction, j],
            device_id={"tp": right if direction == 0 else left}, device_id_type=MESH,
        )

    def unit_copies(k):
        kind, seq = UNITS[k]
        ix = seq if kind[2] == "1" else 4 + seq
        if kind[:2] == "rs":
            p = ix % 3
            routes = (
                ((opp, 0), (right, 1), (right, 0)),
                ((opp, 1), (left, 0), (left, 1)),
            )
            return [
                [
                    remote(part.at[p, half_rows(*routes[d][j]), :], rbuf.at[ix, d, j], k, d, j)
                    for j in range(3)
                ]
                for d in range(2)
            ]
        routes = (
            ((me, 0), (me, 1), (left, 0)),
            ((me, 1), (me, 0), (right, 1)),
        )
        return [
            [
                remote(
                    gath.at[ix, half_rows(*routes[d][j]), :], gath.at[ix, half_rows(*routes[d][j]), :], k, d, j
                )
                for j in range(3)
            ]
            for d in range(2)
        ]

    copies = [unit_copies(k) for k in range(len(UNITS))]

    def begin(k):
        for j in range(2):
            for d in range(2):
                copies[k][d][j].start()

    def middle(k):
        kind, seq = UNITS[k]
        ix = seq if kind[2] == "1" else 4 + seq
        for d in range(2):
            copies[k][d][0].wait_recv()
            if kind[:2] == "rs":
                rows = half_rows(right if d == 0 else left, d)
                part[ix % 3, rows, :] = part[ix % 3, rows, :] + rbuf[ix, d, 0]
            copies[k][d][2].start()

    def finish(k):
        kind, seq = UNITS[k]
        ix = seq if kind[2] == "1" else 4 + seq
        for d in range(2):
            for j in (1, 2):
                copies[k][d][j].wait_recv()
        if kind[:2] == "rs":
            for w in range(2):
                rows = half_rows(me, w)
                total = part[ix % 3, rows, :] + rbuf[ix, w, 2] + rbuf[ix, 1 - w, 1]
                mine = pl.ds(w * half, half)
                mid = (xmid[seq, mine, :].astype(jnp.float32) + total).astype(jnp.bfloat16)
                if kind == "rs1":
                    xmid[seq, mine, :] = mid
                    gath[ix, rows, :] = norm_rows(mid.astype(jnp.float32), 1).astype(jnp.float32)
                else:
                    gath[ix, rows, :] = mid.astype(jnp.float32)
        elif kind == "ag1":
            def cast(i, carry):
                cols = pl.ds(pl.multiple_of(i * TILE, TILE), TILE)
                got = gath[ix, :, cols]
                mean = jnp.sum(got, axis=0, keepdims=True) * (1.0 / n_seq)
                esq[:, cols] += mean * mean
                hmid[:, cols] = got.astype(jnp.bfloat16)
                return carry

            lax.fori_loop(0, width // TILE, cast, 0)
        else:
            if seq >= 2:
                y_copy(seq - 2).wait()

            def store(i, carry):
                cols = pl.ds(pl.multiple_of(i * TILE, TILE), TILE)
                ystage[seq % 2, :, cols] = gath[ix, :, cols].astype(jnp.bfloat16)
                return carry

            lax.fori_loop(0, width // TILE, store, 0)
            y_copy(seq).start()
        for d in range(2):
            for j in range(3):
                copies[k][d][j].wait_send()

    def y_copy(seq):
        return pltpu.make_async_copy(ystage.at[seq % 2], y_ref.at[seq], ysem.at[seq % 2])

    def score_copy(i):
        return pltpu.make_async_remote_copy(
            src_ref=sbuf.at[i], dst_ref=xbuf.at[i], send_sem=xssem.at[i], recv_sem=xrsem.at[i],
            device_id={"dp": partners[i]}, device_id_type=MESH,
        )

    def score_begin():
        n_rows, e_rows = nsq.shape[1] // 128, width // 128
        for r in range(n_rows):
            sbuf[0, r : r + 1, :] = nsq[:, r * 128 : (r + 1) * 128]
        for r in range(e_rows):
            sbuf[0, n_rows + r : n_rows + r + 1, :] = esq[:, r * 128 : (r + 1) * 128]
        sbuf[0, n_rows + e_rows :, :] = jnp.broadcast_to(hsq[...], (8, 128))
        score_copy(0).start()

    def score_step(i):
        score_copy(i).wait()
        sbuf[i + 1] = sbuf[i] + xbuf[i]
        if i + 1 < len(partners):
            score_copy(i + 1).start()

    seq_copy(0).start()
    prefetch(pieces[0])
    seq_copy(1).start()
    hid_copies = [
        pltpu.make_async_copy(
            hid_ref.at[seq, pl.ds(pl.multiple_of(me * blk, blk), blk), :], xmid.at[seq], hsem.at[seq]
        )
        for seq in range(hid_ref.shape[0])
    ]
    for copy in hid_copies:
        copy.start()
    nsq[...] = jnp.zeros_like(nsq)
    esq[...] = jnp.zeros_like(esq)
    hsq[...] = jnp.zeros_like(hsq)

    barrier = pltpu.get_barrier_semaphore()
    for t in (left, right):
        pl.semaphore_signal(barrier, inc=1, device_id={"tp": t}, device_id_type=MESH)
    for other in partners:
        pl.semaphore_signal(barrier, inc=1, device_id={"dp": other}, device_id_type=MESH)
    pl.semaphore_wait(barrier, 2 + len(partners))

    run_piece(HEAD_PIECES[0])
    run_piece(HEAD_PIECES[1])
    begin(0)
    first_means()
    for copy in hid_copies:
        copy.wait()
    for piece in HEAD_PIECES[2:]:
        run_piece(piece)
    first_means()
    last = len(UNITS) - 1
    for k in range(len(UNITS)):
        if k > 0:
            finish(k - 1)
        if k < last:
            begin(k + 1)
        middle(k)
        for piece in SLOT_PIECES.get(k, ()):
            run_piece(piece)
            if piece[0] == "o":
                first_means()
        if k == 10:
            score_begin()
        elif k > 10:
            score_step(k - 11)
    finish(last)
    for i in range(last - 10, len(partners)):
        score_step(i)
    score_ref[...] = jnp.sqrt(sbuf[len(partners)])
    for seq in (2, 3):
        y_copy(seq).wait()


def solution(mesh):
    n_tp = mesh.shape["tp"]
    n_dp = mesh.shape["dp"]

    def local_layer(hidden, positions, ln1_gain, ln1_bias, w_q, w_k, w_v, w_o, ln2_gain, ln2_bias, w_up, w_down):
        n_batch, n_seq, width = hidden.shape
        ff_local = w_up.shape[1]
        heads_local = w_q.shape[1] // HEAD_DIM
        cos_l, sin_l = rope_lanes(positions)
        norm_rows = jnp.stack([
            1.0 + ln1_gain.astype(jnp.float32), ln1_bias.astype(jnp.float32),
            1.0 + ln2_gain.astype(jnp.float32), ln2_bias.astype(jnp.float32),
        ])
        n_rows, e_rows = ff_local // 128, width // 128
        score_rows = n_rows + e_rows + 8
        n_stage = n_dp.bit_length() - 1
        blk = n_seq // n_tp
        any_spec = pl.BlockSpec(memory_space=pl.ANY)
        vmem_spec = pl.BlockSpec(memory_space=pltpu.VMEM)
        n_units = len(UNITS)
        y, score = pl.pallas_call(
            functools.partial(layer_kernel, n_tp, n_dp),
            out_shape=(
                jax.ShapeDtypeStruct(hidden.shape, jnp.bfloat16),
                jax.ShapeDtypeStruct((score_rows, 128), jnp.float32),
            ),
            in_specs=[vmem_spec] * 3 + [any_spec] * 7,
            out_specs=(any_spec, vmem_spec),
            scratch_shapes=[
                pltpu.VMEM((NSLOT, width, TILE), jnp.bfloat16),
                pltpu.VMEM((3, n_seq, width), jnp.float32),
                pltpu.VMEM((2 * n_batch, 2, 3, blk // 2, width), jnp.float32),
                pltpu.VMEM((2 * n_batch, n_seq, width), jnp.float32),
                pltpu.VMEM((n_seq, width), jnp.bfloat16),
                pltpu.VMEM((n_seq, ff_local), jnp.bfloat16),
                pltpu.VMEM((n_batch, blk, width), jnp.bfloat16),
                pltpu.VMEM((2, n_seq, width), jnp.bfloat16),
                pltpu.VMEM((1, ff_local), jnp.float32),
                pltpu.VMEM((1, width), jnp.float32),
                pltpu.VMEM((1, 128), jnp.float32),
                pltpu.VMEM((n_stage + 1, score_rows, 128), jnp.float32),
                pltpu.VMEM((n_stage, score_rows, 128), jnp.float32),
                pltpu.SemaphoreType.DMA((NSLOT,)),
                pltpu.SemaphoreType.DMA,
                pltpu.SemaphoreType.DMA((n_units, 2, 3)),
                pltpu.SemaphoreType.DMA((n_units, 2, 3)),
                pltpu.SemaphoreType.DMA((n_batch,)),
                pltpu.SemaphoreType.DMA((2,)),
                pltpu.SemaphoreType.DMA((2,)),
                pltpu.SemaphoreType.DMA((n_stage,)),
                pltpu.SemaphoreType.DMA((n_stage,)),
            ],
            compiler_params=pltpu.CompilerParams(
                collective_id=0, has_side_effects=True, vmem_limit_bytes=66_000_000
            ),
            name="layer",
        )(cos_l, sin_l, norm_rows, hidden, w_q, w_k, w_v, w_o, w_up, w_down)
        f_neuron = score[:n_rows].reshape(ff_local)
        f_embed = score[n_rows : n_rows + e_rows].reshape(width)
        f_head = score[n_rows + e_rows, :heads_local]
        return y, f_neuron, f_head, f_embed

    weight_col = P(None, "tp")
    weight_row = P("tp", None)
    return jax.shard_map(
        local_layer,
        mesh=mesh,
        in_specs=(P("dp"), P(), P(), P(), weight_col, weight_col, weight_col, weight_row, P(), P(), weight_col, weight_row),
        out_specs=(P("dp"), P("tp"), P("tp"), P()),
        check_vma=False,
    )
```

time: 346 us -> 332 us (0.960)
  the two profiles are of different devices: /device:TPU:32 before, /device:TPU:0 now
where the time goes in v2:
time: 332 us
  Pallas kernels  319 us (96%)
  local copies, waits for them, and re-layouts  7.24 us (2%)
  other arithmetic  5.12 us (2%)
    pallas_call x1, Pallas kernels, local_layer(): pl.pallas_call(functools.partial(layer_kernel, n_tp, n_dp), out_shape=(ja...  319 us

profile of v2, /device:TPU:0, one launch (start us, length us, event | category | flops | bytes accessed | tf_op | source)
XLA Modules:
  0.0 331.6 jit_solution(747273451239869154)
XLA Ops:
  0.6 0.7 convert_element_type.18
  1.3 1.0 fusion.2
  2.3 0.7 convert_add_fusion.1
  3.0 0.7 stack.28
  3.7 0.7 convert_add_fusion
  4.4 0.7 stack.29
  5.1 0.7 pad_maximum_fusion.norm_ref
  5.8 318.6 %layer.1 = (bf16[4,128,4096]{2,1,0:T(8,128)(2,1)}, f32[72,128]{1,0:T(8,128)}) custom-call(f32[128,128]{1,0:T(8,128)} %get-tuple-element.11.cos_ref, f32[128,128]{1,0:T(8,128)} %get-tuple-element.10.sin_ref, f32[4,4096]{1,0:T(4,128)} %pad_maximum_fusion.norm_ref, bf16[4,128,4096]{2,1,0:T(8,128)(2,1)} %hid_ref.1, bf16[4096,1536]{1,0:T(8,128)(2,1)} %wq_ref.1, ...), custom_call_target="tpu_custom_call" | custom-call | tf_op jit(solution)/shard_map/layer/pallas_call | solution.py:432
  324.4 1.3 slice_bitcast_fusion
  325.8 1.2 slice_bitcast_fusion.2
  326.9 4.7 %copy.17 = bf16[4,128,4096]{2,1,0:T(8,128)(2,1)} copy(bf16[4,128,4096]{2,1,0:T(8,128)(2,1)} %get-tuple-element.18) | data formatting | bytes 8388608
  (2 shorter events, 0.0 us)

commit v3 on v2

--- a/solution.py
+++ b/solution.py
@@ -2,6 +2,7 @@
 
 import jax
 import jax.numpy as jnp
+import numpy as np
 from jax import lax
 from jax.experimental import pallas as pl
 from jax.experimental.pallas import tpu as pltpu
@@ -15,32 +16,41 @@
 NSLOT = 3
 MESH = pl.DeviceIdType.MESH
 
-UNITS = (
-    ("rs1", 0), ("rs1", 1), ("ag1", 0), ("rs1", 2), ("ag1", 1), ("rs1", 3), ("rs2", 0), ("ag1", 2),
-    ("rs2", 1), ("ag1", 3), ("ag2", 0), ("rs2", 2), ("ag2", 1), ("rs2", 3), ("ag2", 2), ("ag2", 3),
+PROGRAM = (
+    ("qkv", 0, 0), ("att", 0, 0), ("o", 0, 0), ("o", 0, 1), ("begin", "rs1", 0), ("mean", 0, 0), ("qkv", 1, 0),
+    ("att", 1, 0), ("mid", "rs1", 0), ("o", 1, 0), ("o", 1, 1), ("begin", "rs1", 1), ("mean", 1, 0), ("qkv", 2, 0),
+    ("fin", "rs1", 0), ("begin", "ag1", 0), ("att", 2, 0), ("mid", "rs1", 1), ("o", 2, 0), ("o", 2, 1),
+    ("begin", "rs1", 2), ("mean", 2, 0), ("qkv", 3, 0), ("mid", "ag1", 0), ("att", 3, 0), ("o", 3, 0),
+    ("fin", "rs1", 1), ("begin", "ag1", 1), ("o", 3, 1), ("begin", "rs1", 3), ("mean", 3, 0), ("mid", "rs1", 2),
+    ("fin", "ag1", 0), ("up", 0, 0), ("mid", "ag1", 1), ("up", 0, 1), ("dn", 0, 0), ("dn", 0, 1), ("mid", "rs1", 3),
+    ("begin", "rs2", 0), ("fin", "rs1", 2), ("begin", "ag1", 2), ("fin", "ag1", 1), ("up", 1, 0), ("fin", "rs1", 3),
+    ("begin", "ag1", 3), ("up", 1, 1), ("mid", "rs2", 0), ("dn", 1, 0), ("dn", 1, 1), ("mid", "ag1", 2),
+    ("begin", "rs2", 1), ("mid", "ag1", 3), ("fin", "rs2", 0), ("begin", "ag2", 0), ("fin", "ag1", 2), ("up", 2, 0),
+    ("mid", "rs2", 1), ("up", 2, 1), ("dn", 2, 0), ("dn", 2, 1), ("fin", "ag1", 3), ("begin", "rs2", 2),
+    ("up", 3, 0), ("mid", "ag2", 0), ("up", 3, 1), ("score", 0, 0), ("dn", 3, 0), ("fin", "rs2", 1),
+    ("begin", "ag2", 1), ("dn", 3, 1), ("score", 1, 0), ("mid", "rs2", 2), ("begin", "rs2", 3), ("score", 2, 0),
+    ("fin", "ag2", 0), ("mid", "ag2", 1), ("fin", "rs2", 2), ("score", 3, 0), ("begin", "ag2", 2), ("mid", "rs2", 3),
+    ("fin", "ag2", 1), ("score", 4, 0), ("mid", "ag2", 2), ("fin", "rs2", 3), ("score", 5, 0), ("begin", "ag2", 3),
+    ("fin", "ag2", 2), ("mid", "ag2", 3), ("fin", "ag2", 3),
 )
-HEAD_PIECES = (("qkv", 0), ("o", 0), ("qkv", 1), ("o", 1))
-SLOT_PIECES = {
-    0: (("qkv", 2), ("o", 2)), 2: (("qkv", 3), ("o", 3)), 3: (("up", 0),), 4: (("dn", 0),), 5: (("up", 1),), 6: (("dn", 1),),
-    8: (("up", 2),), 9: (("dn", 2),), 10: (("up", 3),), 11: (("dn", 3),),
-}
+UNITS = tuple((op[1], op[2]) for op in PROGRAM if op[0] == "begin")
+N_TILES = {"qkv": 4, "o": 2, "up": 4, "dn": 4}
 
 
 def rope_lanes(positions):
     half_rot = ROT_DIM // 2
-    lane = jnp.arange(HEAD_DIM)
-    inv_freq = ROPE_BASE ** (-2.0 * (lane % half_rot).astype(jnp.float32) / ROT_DIM)
+    lane = np.arange(HEAD_DIM)
+    inv_freq = np.where(lane < ROT_DIM, ROPE_BASE ** (-2.0 * (lane % half_rot) / ROT_DIM), 0.0).astype(np.float32)
+    sign = np.where(lane < half_rot, -1.0, 1.0).astype(np.float32)
     angle = positions.astype(jnp.float32)[:, None] * inv_freq[None, :]
-    sign = jnp.where(lane < half_rot, -1.0, 1.0)
-    cos_l = jnp.where(lane < ROT_DIM, jnp.cos(angle), 1.0)
-    sin_l = jnp.where(lane < ROT_DIM, sign * jnp.sin(angle), 0.0)
-    return cos_l, sin_l
+    return jnp.cos(angle), sign[None, :] * jnp.sin(angle)
 
 
 def layer_kernel(
-    n_tp, n_dp, cos_ref, sin_ref, norm_ref, hid_ref, wq_ref, wk_ref, wv_ref, wo_ref, wup_ref, wdn_ref,
+    n_tp, n_dp, cos_ref, sin_ref, gain1_ref, bias1_ref, gain2_ref, bias2_ref,
+    hid_ref, wq_ref, wk_ref, wv_ref, wo_ref, wup_ref, wdn_ref,
     y_ref, score_ref,
-    wbuf, part, rbuf, gath, hmid, act, xmid, ystage, nsq, esq, hsq, sbuf, xbuf,
+    wbuf, part, rbuf, gath, hin, qkv, attn, hmid, act, xmid, ystage, norm_ref, nsq, esq, hsq, sbuf, xbuf,
     wsem, vsem, ssem, rsem, hsem, xsem, ysem, xssem, xrsem,
 ):
     me = lax.axis_index("tp")
@@ -63,62 +73,71 @@
     def half_rows(owner, which):
         return pl.ds(pl.multiple_of(owner * blk + which * half, half), half)
 
-    pieces = list(HEAD_PIECES)
-    for k in range(len(UNITS)):
-        pieces.extend(SLOT_PIECES.get(k, ()))
-
+    pieces = [op for op in PROGRAM if op[0] in N_TILES]
     n_q = wq_ref.shape[1]
     n_kv = wk_ref.shape[1]
     n_qkv = n_q + 2 * n_kv
     q_tiles = n_q // TILE
     group = n_q // n_kv
-
-    def n_tiles(kind):
-        if kind == "qkv":
-            return q_tiles + 1
-        return (wup_ref if kind == "up" else wdn_ref).shape[1] // TILE
-
     bases = {}
     base = 0
     for piece in pieces:
         bases[piece] = base
-        base += n_tiles(piece[0])
+        base += N_TILES[piece[0]]
 
     def tile_slot(piece, i):
         return lax.rem(bases[piece] + i, NSLOT)
 
-    def tile_copy(piece, i):
+    def columns(i):
+        return pl.ds(pl.multiple_of(i * TILE, TILE), TILE)
+
+    def tile_copies(piece, i):
+        kind, _, part_no = piece
         slot = tile_slot(piece, i)
-        cols = pl.ds(pl.multiple_of(i * TILE, TILE), TILE)
-        if piece[0] == "o":
-            return pltpu.make_async_copy(wo_ref.at[:, cols], wbuf.at[slot, pl.ds(0, k_o), :], wsem.at[slot])
-        src = {"qkv": wq_ref, "up": wup_ref, "dn": wdn_ref}[piece[0]]
-        return pltpu.make_async_copy(src.at[:, cols], wbuf.at[slot], wsem.at[slot])
+        if kind == "o":
+            first = 2 * (N_TILES[kind] * part_no + i)
+            return (
+                pltpu.make_async_copy(wo_ref.at[:, columns(first)], wbuf.at[slot, pl.ds(0, k_o), :], wsem.at[slot]),
+                pltpu.make_async_copy(
+                    wo_ref.at[:, columns(first + 1)], wbuf.at[slot, pl.ds(k_o, k_o), :], vsem.at[slot]
+                ),
+            )
+        src = {"qkv": wq_ref, "up": wup_ref, "dn": wdn_ref}[kind]
+        tile = N_TILES[kind] * part_no + i
+        return (pltpu.make_async_copy(src.at[:, columns(tile)], wbuf.at[slot], wsem.at[slot]),)
 
     def kv_copies(piece):
         slot = tile_slot(piece, q_tiles)
         return (
             pltpu.make_async_copy(wk_ref, wbuf.at[slot, :, pl.ds(0, n_kv)], wsem.at[slot]),
-            pltpu.make_async_copy(wv_ref, wbuf.at[slot, :, pl.ds(n_kv, n_kv)], vsem),
+            pltpu.make_async_copy(wv_ref, wbuf.at[slot, :, pl.ds(n_kv, n_kv)], vsem.at[slot]),
         )
 
-    def start_tile(piece, i):
-        if piece[0] != "qkv":
-            tile_copy(piece, i).start()
-            return
-
-        @pl.when(i < q_tiles)
-        def _():
-            tile_copy(piece, i).start()
-
-        @pl.when(i == q_tiles)
-        def _():
-            for copy in kv_copies(piece):
-                copy.start()
-
-    def prefetch(piece):
-        for i in range(NSLOT - 1):
-            tile_copy(piece, i).start()
+    def start_all(copies_of_tile):
+        for copy in copies_of_tile:
+            copy.start()
+
+    def look_ahead(piece, i):
+        tiles = N_TILES[piece[0]]
+        after = pieces.index(piece) + 1
+        following = pieces[after] if after < len(pieces) else None
+        static = isinstance(i, int)
+
+        def when(cond, do):
+            if static:
+                if cond:
+                    do()
+            else:
+                pl.when(cond)(do)
+
+        if piece[0] == "qkv":
+            when(i + 2 < q_tiles, lambda: start_all(tile_copies(piece, i + 2)))
+            when(i + 2 == q_tiles, lambda: start_all(kv_copies(piece)))
+        else:
+            when(i + 2 < tiles, lambda: start_all(tile_copies(piece, i + 2)))
+        if following is not None:
+            for j in range(2):
+                when(i == tiles - 2 + j, lambda j=j: start_all(tile_copies(following, j)))
 
     def norm_rows(rows, which):
         mean = jnp.sum(rows, axis=-1, keepdims=True) * (1.0 / width)
@@ -136,7 +155,7 @@
 
         def rows_body(i, carry):
             rows = pl.ds(pl.multiple_of(i * 16, 16), 16)
-            hmid[rows, :] = norm_rows(ystage[seq % 2, rows, :].astype(jnp.float32), 0)
+            hin[rows, :] = norm_rows(ystage[seq % 2, rows, :].astype(jnp.float32), 0)
             return carry
 
         lax.fori_loop(0, n_seq // 16, rows_body, 0)
@@ -146,7 +165,7 @@
     def first_means():
         def cols_body(i, carry):
             cols = pl.ds(pl.multiple_of(i * TILE, TILE), TILE)
-            mean = jnp.sum(hmid[:, cols].astype(jnp.float32), axis=0, keepdims=True) * (1.0 / n_seq)
+            mean = jnp.sum(hin[:, cols].astype(jnp.float32), axis=0, keepdims=True) * (1.0 / n_seq)
             esq[:, cols] += mean * mean
             return carry
 
@@ -170,71 +189,75 @@
             def head_cols(start):
                 return pl.ds(pl.multiple_of(start, HEAD_DIM), HEAD_DIM)
 
-            keys = rotate(act[:, head_cols(n_q + g * HEAD_DIM)], lane)
-            vals = act[:, head_cols(n_q + n_kv + g * HEAD_DIM)]
+            keys = rotate(qkv[:, head_cols(n_q + g * HEAD_DIM)], lane)
+            vals = qkv[:, head_cols(n_q + n_kv + g * HEAD_DIM)]
+            queries = jnp.concatenate(
+                [rotate(qkv[:, head_cols((g * group + i) * HEAD_DIM)], lane) for i in range(group)], axis=0
+            )
+            scores = lax.dot_general(
+                queries, keys, (((1,), (1,)), ((), ())), preferred_element_type=jnp.float32
+            ) * HEAD_DIM ** -0.5
+            probs = []
             for i in range(group):
-                head = g * group + i
-                query = rotate(act[:, head_cols(head * HEAD_DIM)], lane)
-                scores = lax.dot_general(
-                    query, keys, (((1,), (1,)), ((), ())), preferred_element_type=jnp.float32
-                ) * HEAD_DIM ** -0.5
-                scores = jnp.where(row >= col, scores, -1e30)
-                top = jnp.max(scores, axis=-1, keepdims=True)
-                exps = jnp.exp(scores - top)
-                prob = (exps * (1.0 / jnp.sum(exps, axis=-1, keepdims=True))).astype(jnp.bfloat16)
-                out = jnp.dot(prob, vals, preferred_element_type=jnp.float32).astype(jnp.bfloat16)
-                act[:, head_cols(n_qkv + head * HEAD_DIM)] = out
+                masked = jnp.where(row >= col, scores[i * n_seq : (i + 1) * n_seq], -1e30)
+                exps = jnp.exp(masked - jnp.max(masked, axis=-1, keepdims=True))
+                probs.append((exps * (1.0 / jnp.sum(exps, axis=-1, keepdims=True))).astype(jnp.bfloat16))
+            outs = jnp.dot(
+                jnp.concatenate(probs, axis=0), vals, preferred_element_type=jnp.float32
+            ).astype(jnp.bfloat16)
+            head_sum = jnp.zeros((1, HEAD_DIM), jnp.float32)
+            for i in range(group):
+                out = outs[i * n_seq : (i + 1) * n_seq]
+                attn[:, head_cols((g * group + i) * HEAD_DIM)] = out
                 out32 = out.astype(jnp.float32)
                 norm = jnp.sqrt(jnp.sum(out32 * out32, axis=-1, keepdims=True))
                 mean = jnp.sum(norm, axis=0, keepdims=True) * (1.0 / n_seq)
-                hsq[...] += jnp.where(lane_row == head, mean * mean, 0.0)
+                head_sum += jnp.where(lane_row == g * group + i, mean * mean, 0.0)
+            hsq[...] += head_sum
             return carry
 
         lax.fori_loop(0, n_kv // HEAD_DIM, group_body, 0)
 
     def run_piece(piece):
-        kind, seq = piece
-        tiles = n_tiles(kind)
+        kind, seq, part_no = piece
         if kind == "qkv":
             first_norm(seq)
 
         def body(i, carry):
-            tile_copy(piece, i).wait()
-
-            @pl.when(i + NSLOT - 1 < tiles)
-            def _():
-                start_tile(piece, i + NSLOT - 1)
-
+            for copy in tile_copies(piece, i):
+                copy.wait()
+            look_ahead(piece, i)
             slot = tile_slot(piece, i)
-            cols = pl.ds(pl.multiple_of(i * TILE, TILE), TILE)
+            tile = N_TILES[kind] * part_no + i
             if kind == "qkv":
-                act[:, cols] = jnp.dot(hmid[...], wbuf[slot], preferred_element_type=jnp.float32).astype(jnp.bfloat16)
+                qkv[:, columns(i)] = jnp.dot(
+                    hin[...], wbuf[slot], preferred_element_type=jnp.float32
+                ).astype(jnp.bfloat16)
             elif kind == "o":
-                part[seq % 3, :, cols] = jnp.dot(
-                    act[:, pl.ds(n_qkv, n_q)], wbuf[slot, pl.ds(0, k_o), :], preferred_element_type=jnp.float32
-                )
+                for j in range(2):
+                    part[seq % 3, :, columns(2 * tile + j)] = jnp.dot(
+                        attn[...], wbuf[slot, pl.ds(j * k_o, k_o), :], preferred_element_type=jnp.float32
+                    )
             elif kind == "up":
                 up = jnp.maximum(jnp.dot(hmid[...], wbuf[slot], preferred_element_type=jnp.float32), 0.0)
                 sq = up * up
                 mean = jnp.sum(sq, axis=0, keepdims=True) * (1.0 / n_seq)
-                nsq[:, cols] += mean * mean
-                act[:, cols] = sq.astype(jnp.bfloat16)
+                nsq[:, columns(tile)] += mean * mean
+                act[:, columns(tile)] = sq.astype(jnp.bfloat16)
             else:
-                part[(4 + seq) % 3, :, cols] = jnp.dot(act[...], wbuf[slot], preferred_element_type=jnp.float32)
+                part[(4 + seq) % 3, :, columns(tile)] = jnp.dot(
+                    act[...], wbuf[slot], preferred_element_type=jnp.float32
+                )
             return carry
 
-        lax.fori_loop(0, q_tiles if kind == "qkv" else tiles, body, 0)
+        lax.fori_loop(0, q_tiles if kind == "qkv" else N_TILES[kind], body, 0)
         if kind == "qkv":
             for copy in kv_copies(piece):
                 copy.wait()
-            act[:, pl.ds(n_q, 2 * n_kv)] = jnp.dot(
-                hmid[...], wbuf[tile_slot(piece, q_tiles)], preferred_element_type=jnp.float32
+            look_ahead(piece, q_tiles)
+            qkv[:, pl.ds(n_q, 2 * n_kv)] = jnp.dot(
+                hin[...], wbuf[tile_slot(piece, q_tiles)], preferred_element_type=jnp.float32
             ).astype(jnp.bfloat16)
-        after = pieces.index(piece) + 1
-        if after < len(pieces):
-            prefetch(pieces[after])
-        if kind == "qkv":
-            attend()
 
     def remote(src, dst, k, direction, j):
         return pltpu.make_async_remote_copy(
@@ -355,8 +378,17 @@
         if i + 1 < len(partners):
             score_copy(i + 1).start()
 
+    def read_norm(which, gain_ref, bias_ref):
+        gain = 1.0 + gain_ref[...].astype(jnp.float32)
+        bias = bias_ref[...].astype(jnp.float32)
+        for r in range(width // 128):
+            cols = slice(r * 128, (r + 1) * 128)
+            norm_ref[2 * which : 2 * which + 1, cols] = gain[r : r + 1, :]
+            norm_ref[2 * which + 1 : 2 * which + 2, cols] = bias[r : r + 1, :]
+
     seq_copy(0).start()
-    prefetch(pieces[0])
+    for i in range(2):
+        start_all(tile_copies(pieces[0], i))
     seq_copy(1).start()
     hid_copies = [
         pltpu.make_async_copy(
@@ -366,47 +398,61 @@
     ]
     for copy in hid_copies:
         copy.start()
-    nsq[...] = jnp.zeros_like(nsq)
-    esq[...] = jnp.zeros_like(esq)
-    hsq[...] = jnp.zeros_like(hsq)
 
     barrier = pltpu.get_barrier_semaphore()
     for t in (left, right):
         pl.semaphore_signal(barrier, inc=1, device_id={"tp": t}, device_id_type=MESH)
     for other in partners:
         pl.semaphore_signal(barrier, inc=1, device_id={"dp": other}, device_id_type=MESH)
-    pl.semaphore_wait(barrier, 2 + len(partners))
-
-    run_piece(HEAD_PIECES[0])
-    run_piece(HEAD_PIECES[1])
-    begin(0)
-    first_means()
-    for copy in hid_copies:
-        copy.wait()
-    for piece in HEAD_PIECES[2:]:
-        run_piece(piece)
-    first_means()
-    last = len(UNITS) - 1
-    for k in range(len(UNITS)):
-        if k > 0:
-            finish(k - 1)
-        if k < last:
-            begin(k + 1)
-        middle(k)
-        for piece in SLOT_PIECES.get(k, ()):
-            run_piece(piece)
-            if piece[0] == "o":
-                first_means()
-        if k == 10:
+    read_norm(0, gain1_ref, bias1_ref)
+    nsq[...] = jnp.zeros_like(nsq)
+    esq[...] = jnp.zeros_like(esq)
+    hsq[...] = jnp.zeros_like(hsq)
+
+    for op in PROGRAM:
+        name, arg, no = op
+        if name in N_TILES:
+            run_piece(op)
+        elif name == "att":
+            attend()
+        elif name == "mean":
+            first_means()
+        elif name == "begin":
+            k = UNITS.index((arg, no))
+            if k == 0:
+                pl.semaphore_wait(barrier, 2 + len(partners))
+            begin(k)
+            if k == 0:
+                read_norm(1, gain2_ref, bias2_ref)
+                for copy in hid_copies:
+                    copy.wait()
+        elif name == "mid":
+            middle(UNITS.index((arg, no)))
+        elif name == "fin":
+            finish(UNITS.index((arg, no)))
+        elif arg == 0:
             score_begin()
-        elif k > 10:
-            score_step(k - 11)
-    finish(last)
-    for i in range(last - 10, len(partners)):
-        score_step(i)
+        else:
+            score_step(arg - 1)
     score_ref[...] = jnp.sqrt(sbuf[len(partners)])
     for seq in (2, 3):
         y_copy(seq).wait()
+
+
+def final_kernel(n_rows, e_rows, y_ref, score_ref, out_ref, neuron_ref, embed_ref, head_ref, stage, in_sem, out_sem):
+    n_batch = y_ref.shape[0]
+    loads = [pltpu.make_async_copy(y_ref.at[i], stage.at[i], in_sem.at[i]) for i in range(n_batch)]
+    stores = [pltpu.make_async_copy(stage.at[i], out_ref.at[i], out_sem.at[i]) for i in range(n_batch)]
+    for load in loads:
+        load.start()
+    neuron_ref[...] = score_ref[:n_rows, :]
+    embed_ref[...] = score_ref[n_rows : n_rows + e_rows, :]
+    head_ref[...] = score_ref[n_rows + e_rows : n_rows + e_rows + 1, : head_ref.shape[1]]
+    for load, store in zip(loads, stores):
+        load.wait()
+        store.start()
+    for store in stores:
+        store.wait()
 
 
 def solution(mesh):
@@ -418,10 +464,7 @@
         ff_local = w_up.shape[1]
         heads_local = w_q.shape[1] // HEAD_DIM
         cos_l, sin_l = rope_lanes(positions)
-        norm_rows = jnp.stack([
-            1.0 + ln1_gain.astype(jnp.float32), ln1_bias.astype(jnp.float32),
-            1.0 + ln2_gain.astype(jnp.float32), ln2_bias.astype(jnp.float32),
-        ])
+        norm_params = [p.reshape(width // 128, 128) for p in (ln1_gain, ln1_bias, ln2_gain, ln2_bias)]
         n_rows, e_rows = ff_local // 128, width // 128
         score_rows = n_rows + e_rows + 8
         n_stage = n_dp.bit_length() - 1
@@ -435,7 +478,7 @@
                 jax.ShapeDtypeStruct(hidden.shape, jnp.bfloat16),
                 jax.ShapeDtypeStruct((score_rows, 128), jnp.float32),
             ),
-            in_specs=[vmem_spec] * 3 + [any_spec] * 7,
+            in_specs=[vmem_spec] * 6 + [any_spec] * 7,
             out_specs=(any_spec, vmem_spec),
             scratch_shapes=[
                 pltpu.VMEM((NSLOT, width, TILE), jnp.bfloat16),
@@ -443,16 +486,20 @@
                 pltpu.VMEM((2 * n_batch, 2, 3, blk // 2, width), jnp.float32),
                 pltpu.VMEM((2 * n_batch, n_seq, width), jnp.float32),
                 pltpu.VMEM((n_seq, width), jnp.bfloat16),
+                pltpu.VMEM((n_seq, w_q.shape[1] + 2 * w_k.shape[1]), jnp.bfloat16),
+                pltpu.VMEM((n_seq, w_q.shape[1]), jnp.bfloat16),
+                pltpu.VMEM((n_seq, width), jnp.bfloat16),
                 pltpu.VMEM((n_seq, ff_local), jnp.bfloat16),
                 pltpu.VMEM((n_batch, blk, width), jnp.bfloat16),
                 pltpu.VMEM((2, n_seq, width), jnp.bfloat16),
+                pltpu.VMEM((4, width), jnp.float32),
                 pltpu.VMEM((1, ff_local), jnp.float32),
                 pltpu.VMEM((1, width), jnp.float32),
                 pltpu.VMEM((1, 128), jnp.float32),
                 pltpu.VMEM((n_stage + 1, score_rows, 128), jnp.float32),
                 pltpu.VMEM((n_stage, score_rows, 128), jnp.float32),
                 pltpu.SemaphoreType.DMA((NSLOT,)),
-                pltpu.SemaphoreType.DMA,
+                pltpu.SemaphoreType.DMA((NSLOT,)),
                 pltpu.SemaphoreType.DMA((n_units, 2, 3)),
                 pltpu.SemaphoreType.DMA((n_units, 2, 3)),
                 pltpu.SemaphoreType.DMA((n_batch,)),
@@ -465,11 +512,25 @@
                 collective_id=0, has_side_effects=True, vmem_limit_bytes=66_000_000
             ),
             name="layer",
-        )(cos_l, sin_l, norm_rows, hidden, w_q, w_k, w_v, w_o, w_up, w_down)
-        f_neuron = score[:n_rows].reshape(ff_local)
-        f_embed = score[n_rows : n_rows + e_rows].reshape(width)
-        f_head = score[n_rows + e_rows, :heads_local]
-        return y, f_neuron, f_head, f_embed
+        )(cos_l, sin_l, *norm_params, hidden, w_q, w_k, w_v, w_o, w_up, w_down)
+        y, neuron, embed, head = pl.pallas_call(
+            functools.partial(final_kernel, n_rows, e_rows),
+            out_shape=(
+                jax.ShapeDtypeStruct(hidden.shape, jnp.bfloat16),
+                jax.ShapeDtypeStruct((n_rows, 128), jnp.float32),
+                jax.ShapeDtypeStruct((e_rows, 128), jnp.float32),
+                jax.ShapeDtypeStruct((1, heads_local), jnp.float32),
+            ),
+            in_specs=[any_spec, vmem_spec],
+            out_specs=(any_spec, vmem_spec, vmem_spec, vmem_spec),
+            scratch_shapes=[
+                pltpu.VMEM(hidden.shape, jnp.bfloat16),
+                pltpu.SemaphoreType.DMA((n_batch,)),
+                pltpu.SemaphoreType.DMA((n_batch,)),
+            ],
+            name="final",
+        )(y, score)
+        return y, neuron.reshape(ff_local), head.reshape(heads_local), embed.reshape(width)
 
     weight_col = P(None, "tp")
     weight_row = P("tp", None)

time: 332 us -> 299 us (0.901)
  the two profiles are of different devices: /device:TPU:0 before, /device:TPU:1 now
where the time goes in v3:
time: 299 us
  Pallas kernels  296 us (99%)
    pallas_call x1, Pallas kernels, local_layer(): pl.pallas_call(functools.partial(layer_kernel, n_tp, n_dp), out_shape=(ja...  291 us

profile of v3, /device:TPU:1, one launch (start us, length us, event | category | flops | bytes accessed | tf_op | source)
XLA Modules:
  0.0 298.8 jit_solution(9124375310261959137)
XLA Ops:
  0.6 0.7 convert_element_type.3
  1.3 1.6 fusion
  2.9 291.0 %layer.1 = (bf16[4,128,4096]{2,1,0:T(8,128)(2,1)}, f32[72,128]{1,0:T(8,128)}) custom-call(f32[128,128]{1,0:T(8,128)} %get-tuple-element.17.cos_ref, f32[128,128]{1,0:T(8,128)} %get-tuple-element.16.sin_ref, bf16[32,128]{1,0:T(8,128)(2,1)} %bitcast.7, bf16[32,128]{1,0:T(8,128)(2,1)} %bitcast.8, bf16[32,128]{1,0:T(8,128)(2,1)} %bitcast.9, ...), custom_call_target="tpu_custom_call" | custom-call | tf_op jit(solution)/shard_map/layer/pallas_call | solution.py:475
  293.9 4.7 %final.1 = (bf16[4,128,4096]{2,1,0:T(8,128)(2,1)}, f32[32,128]{1,0:T(8,128)}, f32[32,128]{1,0:T(8,128)}, f32[1,12]{1,0:T(1,128)}) custom-call(bf16[4,128,4096]{2,1,0:T(8,128)(2,1)} %get-tuple-element.10.y_ref, f32[72,128]{1,0:T(8,128)} %get-tuple-element.11.score_ref), custom_call_target="tpu_custom_call" | custom-call | tf_op jit(solution)/shard_map/final/pallas_call | solution.py:516

commit v4 on v3

--- a/solution.py
+++ b/solution.py
@@ -14,44 +14,43 @@
 LN_EPS = 1e-5
 TILE = 512
 NSLOT = 3
+VMEM_LIMIT = 66_000_000
 MESH = pl.DeviceIdType.MESH
 
 PROGRAM = (
-    ("qkv", 0, 0), ("att", 0, 0), ("o", 0, 0), ("o", 0, 1), ("begin", "rs1", 0), ("mean", 0, 0), ("qkv", 1, 0),
-    ("att", 1, 0), ("mid", "rs1", 0), ("o", 1, 0), ("o", 1, 1), ("begin", "rs1", 1), ("mean", 1, 0), ("qkv", 2, 0),
-    ("fin", "rs1", 0), ("begin", "ag1", 0), ("att", 2, 0), ("mid", "rs1", 1), ("o", 2, 0), ("o", 2, 1),
-    ("begin", "rs1", 2), ("mean", 2, 0), ("qkv", 3, 0), ("mid", "ag1", 0), ("att", 3, 0), ("o", 3, 0),
-    ("fin", "rs1", 1), ("begin", "ag1", 1), ("o", 3, 1), ("begin", "rs1", 3), ("mean", 3, 0), ("mid", "rs1", 2),
-    ("fin", "ag1", 0), ("up", 0, 0), ("mid", "ag1", 1), ("up", 0, 1), ("dn", 0, 0), ("dn", 0, 1), ("mid", "rs1", 3),
-    ("begin", "rs2", 0), ("fin", "rs1", 2), ("begin", "ag1", 2), ("fin", "ag1", 1), ("up", 1, 0), ("fin", "rs1", 3),
-    ("begin", "ag1", 3), ("up", 1, 1), ("mid", "rs2", 0), ("dn", 1, 0), ("dn", 1, 1), ("mid", "ag1", 2),
-    ("begin", "rs2", 1), ("mid", "ag1", 3), ("fin", "rs2", 0), ("begin", "ag2", 0), ("fin", "ag1", 2), ("up", 2, 0),
-    ("mid", "rs2", 1), ("up", 2, 1), ("dn", 2, 0), ("dn", 2, 1), ("fin", "ag1", 3), ("begin", "rs2", 2),
-    ("up", 3, 0), ("mid", "ag2", 0), ("up", 3, 1), ("score", 0, 0), ("dn", 3, 0), ("fin", "rs2", 1),
-    ("begin", "ag2", 1), ("dn", 3, 1), ("score", 1, 0), ("mid", "rs2", 2), ("begin", "rs2", 3), ("score", 2, 0),
-    ("fin", "ag2", 0), ("mid", "ag2", 1), ("fin", "rs2", 2), ("score", 3, 0), ("begin", "ag2", 2), ("mid", "rs2", 3),
-    ("fin", "ag2", 1), ("score", 4, 0), ("mid", "ag2", 2), ("fin", "rs2", 3), ("score", 5, 0), ("begin", "ag2", 3),
-    ("fin", "ag2", 2), ("mid", "ag2", 3), ("fin", "ag2", 3),
+    ("qkv", 0, 0), ("att", 0, 0), ("o", 0, 0), ("early", "rs1", 0), ("o", 0, 1), ("begin", "rs1", 0), ("mean", 0, 0),
+    ("qkv", 1, 0), ("att", 1, 0), ("mid", "rs1", 0), ("o", 1, 0), ("o", 1, 1), ("begin", "rs1", 1), ("mean", 1, 0),
+    ("qkv", 2, 0), ("att", 2, 0), ("fin", "rs1", 0), ("begin", "ag1", 0), ("o", 2, 0), ("o", 2, 1),
+    ("mid", "rs1", 1), ("mean", 2, 0), ("qkv", 3, 0), ("begin", "rs1", 2), ("att", 3, 0), ("o", 3, 0), ("o", 3, 1),
+    ("mid", "ag1", 0), ("mean", 3, 0), ("begin", "rs1", 3), ("fin", "rs1", 1), ("mid", "rs1", 2),
+    ("begin", "ag1", 1), ("fin", "ag1", 0), ("up", 0, 0), ("mid", "rs1", 3), ("up", 0, 1), ("dn", 0, 0),
+    ("dn", 0, 1), ("fin", "rs1", 2), ("mid", "ag1", 1), ("begin", "ag1", 2), ("begin", "rs2", 0), ("fin", "rs1", 3),
+    ("fin", "ag1", 1), ("up", 1, 0), ("mid", "ag1", 2), ("up", 1, 1), ("begin", "ag1", 3), ("dn", 1, 0),
+    ("dn", 1, 1), ("mid", "rs2", 0), ("begin", "rs2", 1), ("fin", "ag1", 2), ("up", 2, 0), ("mid", "ag1", 3),
+    ("up", 2, 1), ("dn", 2, 0), ("dn", 2, 1), ("fin", "rs2", 0), ("mid", "rs2", 1), ("begin", "ag2", 0),
+    ("begin", "rs2", 2), ("fin", "ag1", 3), ("up", 3, 0), ("fin", "rs2", 1), ("up", 3, 1), ("score", 0, 0),
+    ("mid", "ag2", 0), ("dn", 3, 0), ("begin", "ag2", 1), ("score", 1, 0), ("dn", 3, 1), ("mid", "rs2", 2),
+    ("begin", "rs2", 3), ("score", 2, 0), ("fin", "ag2", 0), ("mid", "ag2", 1), ("fin", "rs2", 2), ("score", 3, 0),
+    ("begin", "ag2", 2), ("mid", "rs2", 3), ("fin", "ag2", 1), ("score", 4, 0), ("mid", "ag2", 2), ("fin", "rs2", 3),
+    ("begin", "ag2", 3), ("score", 5, 0), ("fin", "ag2", 2), ("mid", "ag2", 3), ("fin", "ag2", 3),
 )
 UNITS = tuple((op[1], op[2]) for op in PROGRAM if op[0] == "begin")
 N_TILES = {"qkv": 4, "o": 2, "up": 4, "dn": 4}
 
 
-def rope_lanes(positions):
+def rope_rows():
     half_rot = ROT_DIM // 2
     lane = np.arange(HEAD_DIM)
-    inv_freq = np.where(lane < ROT_DIM, ROPE_BASE ** (-2.0 * (lane % half_rot) / ROT_DIM), 0.0).astype(np.float32)
-    sign = np.where(lane < half_rot, -1.0, 1.0).astype(np.float32)
-    angle = positions.astype(jnp.float32)[:, None] * inv_freq[None, :]
-    return jnp.cos(angle), sign[None, :] * jnp.sin(angle)
+    inv_freq = np.where(lane < ROT_DIM, ROPE_BASE ** (-2.0 * (lane % half_rot) / ROT_DIM), 0.0)
+    return np.stack([inv_freq, np.where(lane < half_rot, -1.0, 1.0)]).astype(np.float32)
 
 
 def layer_kernel(
-    n_tp, n_dp, cos_ref, sin_ref, gain1_ref, bias1_ref, gain2_ref, bias2_ref,
+    n_tp, n_dp, pos_in, freq_in, gain1_in, bias1_in, gain2_in, bias2_in,
     hid_ref, wq_ref, wk_ref, wv_ref, wo_ref, wup_ref, wdn_ref,
     y_ref, score_ref,
-    wbuf, part, rbuf, gath, hin, qkv, attn, hmid, act, xmid, ystage, norm_ref, nsq, esq, hsq, sbuf, xbuf,
-    wsem, vsem, ssem, rsem, hsem, xsem, ysem, xssem, xrsem,
+    wbuf, part, rbuf, gath, hin, qkv, attn, hmid, act, xmid, ystage, pos_ref, freq_ref, rope_ref, raw_ref, norm_ref, nsq, esq, hsq, sbuf, xbuf,
+    wsem, vsem, ssem, rsem, esend, erecv, psem, bsem, osem, hsem, xsem, ysem, xssem, xrsem,
 ):
     me = lax.axis_index("tp")
     my_dp = lax.axis_index("dp")
@@ -117,27 +116,22 @@
         for copy in copies_of_tile:
             copy.start()
 
+    def start_tile(number):
+        for piece in pieces:
+            tile = number - bases[piece]
+            if 0 <= tile < N_TILES[piece[0]]:
+                is_kv = piece[0] == "qkv" and tile == q_tiles
+                start_all(kv_copies(piece) if is_kv else tile_copies(piece, tile))
+
     def look_ahead(piece, i):
-        tiles = N_TILES[piece[0]]
-        after = pieces.index(piece) + 1
-        following = pieces[after] if after < len(pieces) else None
-        static = isinstance(i, int)
-
-        def when(cond, do):
-            if static:
-                if cond:
-                    do()
-            else:
-                pl.when(cond)(do)
-
-        if piece[0] == "qkv":
-            when(i + 2 < q_tiles, lambda: start_all(tile_copies(piece, i + 2)))
-            when(i + 2 == q_tiles, lambda: start_all(kv_copies(piece)))
-        else:
-            when(i + 2 < tiles, lambda: start_all(tile_copies(piece, i + 2)))
-        if following is not None:
-            for j in range(2):
-                when(i == tiles - 2 + j, lambda j=j: start_all(tile_copies(following, j)))
+        if isinstance(i, int):
+            start_tile(bases[piece] + i + NSLOT)
+            return
+        for j in range(q_tiles if piece[0] == "qkv" else N_TILES[piece[0]]):
+
+            @pl.when(i == j)
+            def _(j=j):
+                start_tile(bases[piece] + j + NSLOT)
 
     def norm_rows(rows, which):
         mean = jnp.sum(rows, axis=-1, keepdims=True) * (1.0 / width)
@@ -177,7 +171,7 @@
         ahead = pltpu.roll(val, HEAD_DIM - rot_half, 1)
         behind = pltpu.roll(val, rot_half, 1)
         partner = jnp.where(lane < rot_half, ahead, behind)
-        return (val * cos_ref[...] + partner * sin_ref[...]).astype(jnp.bfloat16)
+        return (val * rope_ref[0] + partner * rope_ref[1]).astype(jnp.bfloat16)
 
     def attend():
         lane = lax.broadcasted_iota(jnp.int32, (n_seq, HEAD_DIM), 1)
@@ -226,7 +220,6 @@
         def body(i, carry):
             for copy in tile_copies(piece, i):
                 copy.wait()
-            look_ahead(piece, i)
             slot = tile_slot(piece, i)
             tile = N_TILES[kind] * part_no + i
             if kind == "qkv":
@@ -248,16 +241,17 @@
                 part[(4 + seq) % 3, :, columns(tile)] = jnp.dot(
                     act[...], wbuf[slot], preferred_element_type=jnp.float32
                 )
+            look_ahead(piece, i)
             return carry
 
         lax.fori_loop(0, q_tiles if kind == "qkv" else N_TILES[kind], body, 0)
         if kind == "qkv":
             for copy in kv_copies(piece):
                 copy.wait()
-            look_ahead(piece, q_tiles)
             qkv[:, pl.ds(n_q, 2 * n_kv)] = jnp.dot(
                 hin[...], wbuf[tile_slot(piece, q_tiles)], preferred_element_type=jnp.float32
             ).astype(jnp.bfloat16)
+            look_ahead(piece, q_tiles)
 
     def remote(src, dst, k, direction, j):
         return pltpu.make_async_remote_copy(
@@ -297,6 +291,29 @@
 
     copies = [unit_copies(k) for k in range(len(UNITS))]
 
+    def early_copies():
+        owners = (((opp, 0), (right, 1)), ((opp, 1), (left, 0)))
+
+        def one(d, j, side):
+            cols = pl.ds(side * (width // 2), width // 2)
+            sems = (esend, erecv) if side == 0 else (ssem.at[0], rsem.at[0])
+            return pltpu.make_async_remote_copy(
+                src_ref=part.at[0, half_rows(*owners[d][j]), cols], dst_ref=rbuf.at[0, d, j, :, cols],
+                send_sem=sems[0].at[d, j], recv_sem=sems[1].at[d, j],
+                device_id={"tp": right if d == 0 else left}, device_id_type=MESH,
+            )
+
+        return [[[one(d, j, side) for j in range(2)] for d in range(2)] for side in range(2)]
+
+    early, late = early_copies()
+    for d in range(2):
+        copies[0][d][:2] = late[d]
+
+    def early_begin():
+        for j in range(2):
+            for d in range(2):
+                early[d][j].start()
+
     def begin(k):
         for j in range(2):
             for d in range(2):
@@ -306,6 +323,8 @@
         kind, seq = UNITS[k]
         ix = seq if kind[2] == "1" else 4 + seq
         for d in range(2):
+            if k == 0:
+                early[d][0].wait_recv()
             copies[k][d][0].wait_recv()
             if kind[:2] == "rs":
                 rows = half_rows(right if d == 0 else left, d)
@@ -315,7 +334,12 @@
     def finish(k):
         kind, seq = UNITS[k]
         ix = seq if kind[2] == "1" else 4 + seq
+        if k == len(UNITS) - 1:
+            last_finish(k, seq, ix)
+            return
         for d in range(2):
+            if k == 0:
+                early[d][1].wait_recv()
             for j in (1, 2):
                 copies[k][d][j].wait_recv()
         if kind[:2] == "rs":
@@ -353,6 +377,32 @@
         for d in range(2):
             for j in range(3):
                 copies[k][d][j].wait_send()
+                if k == 0 and j < 2:
+                    early[d][j].wait_send()
+
+    def block_copy(seq, owner, i):
+        rows = pl.ds(pl.multiple_of(owner * blk, blk), blk)
+        return pltpu.make_async_copy(ystage.at[seq % 2, rows, :], y_ref.at[seq, rows, :], bsem.at[i])
+
+    def last_finish(k, seq, ix):
+        y_copy(seq - 2).wait()
+        for i, owner in enumerate((me, left, right, opp)):
+            rows = pl.ds(pl.multiple_of(owner * blk, blk), blk)
+            if i == 1 or i == 3:
+                for d in range(2):
+                    copies[k][d][1 if i == 1 else 2].wait_recv()
+
+            def store(c, carry, rows=rows):
+                ystage[seq % 2, rows, columns(c)] = gath[ix, rows, columns(c)].astype(jnp.bfloat16)
+                return carry
+
+            lax.fori_loop(0, width // TILE, store, 0)
+            block_copy(seq, owner, i).start()
+        for d in range(2):
+            for j in range(3):
+                copies[k][d][j].wait_send()
+        for i, owner in enumerate((me, left, right, opp)):
+            block_copy(seq, owner, i).wait()
 
     def y_copy(seq):
         return pltpu.make_async_copy(ystage.at[seq % 2], y_ref.at[seq], ysem.at[seq % 2])
@@ -378,80 +428,116 @@
         if i + 1 < len(partners):
             score_copy(i + 1).start()
 
-    def read_norm(which, gain_ref, bias_ref):
-        gain = 1.0 + gain_ref[...].astype(jnp.float32)
-        bias = bias_ref[...].astype(jnp.float32)
+    def read_norm(which):
+        for i in (2 * which, 2 * which + 1):
+            param_copies[i].wait()
+        gain = 1.0 + raw_ref[2 * which].astype(jnp.float32)
+        bias = raw_ref[2 * which + 1].astype(jnp.float32)
         for r in range(width // 128):
             cols = slice(r * 128, (r + 1) * 128)
             norm_ref[2 * which : 2 * which + 1, cols] = gain[r : r + 1, :]
             norm_ref[2 * which + 1 : 2 * which + 2, cols] = bias[r : r + 1, :]
 
-    seq_copy(0).start()
-    for i in range(2):
-        start_all(tile_copies(pieces[0], i))
-    seq_copy(1).start()
+    def read_rope():
+        for copy in param_copies[4:]:
+            copy.wait()
+        row = lax.broadcasted_iota(jnp.int32, (n_seq, n_seq), 0)
+        col = lax.broadcasted_iota(jnp.int32, (n_seq, n_seq), 1)
+        pos = jnp.where(row == col, pos_ref[...].astype(jnp.float32), 0.0)
+        angle = jnp.sum(pos, axis=1, keepdims=True) * freq_ref[0:1, :]
+        rope_ref[0] = jnp.cos(angle)
+        rope_ref[1] = freq_ref[1:2, :] * jnp.sin(angle)
+
+    param_copies = [
+        pltpu.make_async_copy(src, raw_ref.at[i], psem.at[i])
+        for i, src in enumerate((gain1_in, bias1_in, gain2_in, bias2_in))
+    ] + [
+        pltpu.make_async_copy(pos_in, pos_ref, psem.at[4]),
+        pltpu.make_async_copy(freq_in, freq_ref, psem.at[5]),
+    ]
     hid_copies = [
         pltpu.make_async_copy(
             hid_ref.at[seq, pl.ds(pl.multiple_of(me * blk, blk), blk), :], xmid.at[seq], hsem.at[seq]
         )
         for seq in range(hid_ref.shape[0])
     ]
-    for copy in hid_copies:
-        copy.start()
+    seq_copy(0).start()
+    start_all(param_copies)
+    start_tile(0)
+    for i in range(1, NSLOT):
+        start_tile(i)
 
     barrier = pltpu.get_barrier_semaphore()
     for t in (left, right):
         pl.semaphore_signal(barrier, inc=1, device_id={"tp": t}, device_id_type=MESH)
     for other in partners:
         pl.semaphore_signal(barrier, inc=1, device_id={"dp": other}, device_id_type=MESH)
-    read_norm(0, gain1_ref, bias1_ref)
+    read_norm(0)
+    read_rope()
     nsq[...] = jnp.zeros_like(nsq)
     esq[...] = jnp.zeros_like(esq)
     hsq[...] = jnp.zeros_like(hsq)
 
+    score_out = pltpu.make_async_copy(sbuf.at[0], score_ref, osem)
     for op in PROGRAM:
         name, arg, no = op
         if name in N_TILES:
             run_piece(op)
         elif name == "att":
+            if arg == 0:
+                seq_copy(1).start()
             attend()
+        elif name == "early":
+            pl.semaphore_wait(barrier, 2 + len(partners))
+            early_begin()
         elif name == "mean":
             first_means()
         elif name == "begin":
             k = UNITS.index((arg, no))
-            if k == 0:
-                pl.semaphore_wait(barrier, 2 + len(partners))
             begin(k)
             if k == 0:
-                read_norm(1, gain2_ref, bias2_ref)
-                for copy in hid_copies:
-                    copy.wait()
+                start_all(hid_copies)
+                read_norm(1)
         elif name == "mid":
             middle(UNITS.index((arg, no)))
         elif name == "fin":
+            if (arg, no) == UNITS[0]:
+                for copy in hid_copies:
+                    copy.wait()
             finish(UNITS.index((arg, no)))
         elif arg == 0:
             score_begin()
         else:
             score_step(arg - 1)
-    score_ref[...] = jnp.sqrt(sbuf[len(partners)])
-    for seq in (2, 3):
-        y_copy(seq).wait()
-
-
-def final_kernel(n_rows, e_rows, y_ref, score_ref, out_ref, neuron_ref, embed_ref, head_ref, stage, in_sem, out_sem):
-    n_batch = y_ref.shape[0]
-    loads = [pltpu.make_async_copy(y_ref.at[i], stage.at[i], in_sem.at[i]) for i in range(n_batch)]
-    stores = [pltpu.make_async_copy(stage.at[i], out_ref.at[i], out_sem.at[i]) for i in range(n_batch)]
+            if arg == len(partners):
+                sbuf[0] = jnp.sqrt(sbuf[len(partners)])
+                score_out.start()
+    y_copy(2).wait()
+    score_out.wait()
+
+
+def final_kernel(
+    n_rows, e_rows, y_ref, score_ref, out_ref, neuron_ref, embed_ref, head_ref, stage, scores, heads, in_sem, out_sem
+):
+    count = y_ref.shape[0]
+    loads = [pltpu.make_async_copy(y_ref.at[i], stage.at[i], in_sem.at[i]) for i in range(count)]
+    stores = [pltpu.make_async_copy(stage.at[i], out_ref.at[i], out_sem.at[i]) for i in range(count)]
+    loads.insert(0, pltpu.make_async_copy(score_ref, scores, in_sem.at[count]))
+    score_stores = [
+        pltpu.make_async_copy(scores.at[pl.ds(0, n_rows), :], neuron_ref, out_sem.at[count]),
+        pltpu.make_async_copy(scores.at[pl.ds(n_rows, e_rows), :], embed_ref, out_sem.at[count + 1]),
+        pltpu.make_async_copy(heads, head_ref, out_sem.at[count + 2]),
+    ]
     for load in loads:
         load.start()
-    neuron_ref[...] = score_ref[:n_rows, :]
-    embed_ref[...] = score_ref[n_rows : n_rows + e_rows, :]
-    head_ref[...] = score_ref[n_rows + e_rows : n_rows + e_rows + 1, : head_ref.shape[1]]
-    for load, store in zip(loads, stores):
+    loads[0].wait()
+    heads[...] = scores[n_rows + e_rows : n_rows + e_rows + 1, : heads.shape[1]]
+    for store in score_stores:
+        store.start()
+    for load, store in zip(loads[1:], stores):
         load.wait()
         store.start()
-    for store in stores:
+    for store in score_stores + stores:
         store.wait()
 
 
@@ -463,14 +549,12 @@
         n_batch, n_seq, width = hidden.shape
         ff_local = w_up.shape[1]
         heads_local = w_q.shape[1] // HEAD_DIM
-        cos_l, sin_l = rope_lanes(positions)
         norm_params = [p.reshape(width // 128, 128) for p in (ln1_gain, ln1_bias, ln2_gain, ln2_bias)]
         n_rows, e_rows = ff_local // 128, width // 128
         score_rows = n_rows + e_rows + 8
         n_stage = n_dp.bit_length() - 1
         blk = n_seq // n_tp
         any_spec = pl.BlockSpec(memory_space=pl.ANY)
-        vmem_spec = pl.BlockSpec(memory_space=pltpu.VMEM)
         n_units = len(UNITS)
         y, score = pl.pallas_call(
             functools.partial(layer_kernel, n_tp, n_dp),
@@ -478,8 +562,8 @@
                 jax.ShapeDtypeStruct(hidden.shape, jnp.bfloat16),
                 jax.ShapeDtypeStruct((score_rows, 128), jnp.float32),
             ),
-            in_specs=[vmem_spec] * 6 + [any_spec] * 7,
-            out_specs=(any_spec, vmem_spec),
+            in_specs=[any_spec] * 13,
+            out_specs=(any_spec, any_spec),
             scratch_shapes=[
                 pltpu.VMEM((NSLOT, width, TILE), jnp.bfloat16),
                 pltpu.VMEM((3, n_seq, width), jnp.float32),
@@ -492,6 +576,10 @@
                 pltpu.VMEM((n_seq, ff_local), jnp.bfloat16),
                 pltpu.VMEM((n_batch, blk, width), jnp.bfloat16),
                 pltpu.VMEM((2, n_seq, width), jnp.bfloat16),
+                pltpu.VMEM((1, n_seq), jnp.int32),
+                pltpu.VMEM((2, HEAD_DIM), jnp.float32),
+                pltpu.VMEM((2, n_seq, HEAD_DIM), jnp.float32),
+                pltpu.VMEM((4, width // 128, 128), jnp.bfloat16),
                 pltpu.VMEM((4, width), jnp.float32),
                 pltpu.VMEM((1, ff_local), jnp.float32),
                 pltpu.VMEM((1, width), jnp.float32),
@@ -502,6 +590,11 @@
                 pltpu.SemaphoreType.DMA((NSLOT,)),
                 pltpu.SemaphoreType.DMA((n_units, 2, 3)),
                 pltpu.SemaphoreType.DMA((n_units, 2, 3)),
+                pltpu.SemaphoreType.DMA((2, 2)),
+                pltpu.SemaphoreType.DMA((2, 2)),
+                pltpu.SemaphoreType.DMA((6,)),
+                pltpu.SemaphoreType.DMA((n_tp,)),
+                pltpu.SemaphoreType.DMA,
                 pltpu.SemaphoreType.DMA((n_batch,)),
                 pltpu.SemaphoreType.DMA((2,)),
                 pltpu.SemaphoreType.DMA((2,)),
@@ -509,10 +602,10 @@
                 pltpu.SemaphoreType.DMA((n_stage,)),
             ],
             compiler_params=pltpu.CompilerParams(
-                collective_id=0, has_side_effects=True, vmem_limit_bytes=66_000_000
+                collective_id=0, has_side_effects=True, vmem_limit_bytes=VMEM_LIMIT
             ),
             name="layer",
-        )(cos_l, sin_l, *norm_params, hidden, w_q, w_k, w_v, w_o, w_up, w_down)
+        )(positions.reshape(1, n_seq), rope_rows(), *norm_params, hidden, w_q, w_k, w_v, w_o, w_up, w_down)
         y, neuron, embed, head = pl.pallas_call(
             functools.partial(final_kernel, n_rows, e_rows),
             out_shape=(
@@ -521,12 +614,14 @@
                 jax.ShapeDtypeStruct((e_rows, 128), jnp.float32),
                 jax.ShapeDtypeStruct((1, heads_local), jnp.float32),
             ),
-            in_specs=[any_spec, vmem_spec],
-            out_specs=(any_spec, vmem_spec, vmem_spec, vmem_spec),
+            in_specs=[any_spec, any_spec],
+            out_specs=(any_spec, any_spec, any_spec, any_spec),
             scratch_shapes=[
                 pltpu.VMEM(hidden.shape, jnp.bfloat16),
-                pltpu.SemaphoreType.DMA((n_batch,)),
-                pltpu.SemaphoreType.DMA((n_batch,)),
+                pltpu.VMEM((score_rows, 128), jnp.float32),
+                pltpu.VMEM((1, heads_local), jnp.float32),
+                pltpu.SemaphoreType.DMA((n_batch + 1,)),
+                pltpu.SemaphoreType.DMA((n_batch + 3,)),
             ],
             name="final",
         )(y, score)

time: 299 us -> 293 us (0.980)
  Pallas kernels: 296 us -> 292 us
where the time goes in v4:
time: 293 us
  Pallas kernels  292 us (100%)
    pallas_call x1, Pallas kernels, local_layer(): pl.pallas_call(functools.partial(layer_kernel, n_tp, n_dp), out_shape=(ja...  289 us

profile of v4, /device:TPU:1, one launch (start us, length us, event | category | flops | bytes accessed | tf_op | source)
XLA Modules:
  0.0 292.8 jit_solution(10166696054318852677)
XLA Ops:
  0.6 288.6 %layer.1 = (bf16[4,128,4096]{2,1,0:T(8,128)(2,1)}, f32[72,128]{1,0:T(8,128)}) custom-call(s32[1,128]{1,0:T(1,128)} %bitcast.12, f32[2,128]{1,0:T(2,128)} %constant.2.clone.freq_in, bf16[32,128]{1,0:T(8,128)(2,1)} %bitcast.8, bf16[32,128]{1,0:T(8,128)(2,1)} %bitcast.9, bf16[32,128]{1,0:T(8,128)(2,1)} %bitcast.10, bf16[32,128]{1,0:T(8,128)(2,1)} %bitcast.11, ...), custom_call_target="tpu_custom_call" | custom-call | tf_op jit(solution)/shard_map/layer/pallas_call | solution.py:559
  289.2 3.4 %final.1 = (bf16[4,128,4096]{2,1,0:T(8,128)(2,1)}, f32[32,128]{1,0:T(8,128)}, f32[32,128]{1,0:T(8,128)}, f32[1,12]{1,0:T(1,128)}) custom-call(bf16[4,128,4096]{2,1,0:T(8,128)(2,1)} %get-tuple-element.10.y_ref, f32[72,128]{1,0:T(8,128)} %get-tuple-element.11.score_ref), custom_call_target="tpu_custom_call" | custom-call | tf_op jit(solution)/shard_map/final/pallas_call | solution.py:609

commit v5 on v4

--- a/solution.py
+++ b/solution.py
@@ -13,7 +13,7 @@
 ROPE_BASE = 10000.0
 LN_EPS = 1e-5
 TILE = 512
-NSLOT = 3
+NSLOT = 4
 VMEM_LIMIT = 66_000_000
 MESH = pl.DeviceIdType.MESH
 
@@ -152,7 +152,7 @@
             hin[rows, :] = norm_rows(ystage[seq % 2, rows, :].astype(jnp.float32), 0)
             return carry
 
-        lax.fori_loop(0, n_seq // 16, rows_body, 0)
+        lax.fori_loop(0, n_seq // 16, rows_body, 0, unroll=4)
         if seq + 2 < hid_ref.shape[0]:
             seq_copy(seq + 2).start()
 
@@ -246,6 +246,8 @@
 
         lax.fori_loop(0, q_tiles if kind == "qkv" else N_TILES[kind], body, 0)
         if kind == "qkv":
+            if seq == 0:
+                read_rope()
             for copy in kv_copies(piece):
                 copy.wait()
             qkv[:, pl.ds(n_q, 2 * n_kv)] = jnp.dot(
@@ -292,27 +294,21 @@
     copies = [unit_copies(k) for k in range(len(UNITS))]
 
     def early_copies():
-        owners = (((opp, 0), (right, 1)), ((opp, 1), (left, 0)))
-
-        def one(d, j, side):
+        def one(d, side):
+            rows = half_rows(opp, d)
             cols = pl.ds(side * (width // 2), width // 2)
-            sems = (esend, erecv) if side == 0 else (ssem.at[0], rsem.at[0])
+            sems = (esend.at[d], erecv.at[d]) if side == 0 else (ssem.at[0, d, 0], rsem.at[0, d, 0])
             return pltpu.make_async_remote_copy(
-                src_ref=part.at[0, half_rows(*owners[d][j]), cols], dst_ref=rbuf.at[0, d, j, :, cols],
-                send_sem=sems[0].at[d, j], recv_sem=sems[1].at[d, j],
+                src_ref=part.at[0, rows, cols], dst_ref=rbuf.at[0, d, 0, :, cols],
+                send_sem=sems[0], recv_sem=sems[1],
                 device_id={"tp": right if d == 0 else left}, device_id_type=MESH,
             )
 
-        return [[[one(d, j, side) for j in range(2)] for d in range(2)] for side in range(2)]
+        return [[one(d, side) for d in range(2)] for side in range(2)]
 
     early, late = early_copies()
     for d in range(2):
-        copies[0][d][:2] = late[d]
-
-    def early_begin():
-        for j in range(2):
-            for d in range(2):
-                early[d][j].start()
+        copies[0][d][0] = late[d]
 
     def begin(k):
         for j in range(2):
@@ -324,7 +320,7 @@
         ix = seq if kind[2] == "1" else 4 + seq
         for d in range(2):
             if k == 0:
-                early[d][0].wait_recv()
+                early[d].wait_recv()
             copies[k][d][0].wait_recv()
             if kind[:2] == "rs":
                 rows = half_rows(right if d == 0 else left, d)
@@ -338,8 +334,6 @@
             last_finish(k, seq, ix)
             return
         for d in range(2):
-            if k == 0:
-                early[d][1].wait_recv()
             for j in (1, 2):
                 copies[k][d][j].wait_recv()
         if kind[:2] == "rs":
@@ -377,8 +371,8 @@
         for d in range(2):
             for j in range(3):
                 copies[k][d][j].wait_send()
-                if k == 0 and j < 2:
-                    early[d][j].wait_send()
+                if k == 0 and j == 0:
+                    early[d].wait_send()
 
     def block_copy(seq, owner, i):
         rows = pl.ds(pl.multiple_of(owner * blk, blk), blk)
@@ -473,7 +467,6 @@
     for other in partners:
         pl.semaphore_signal(barrier, inc=1, device_id={"dp": other}, device_id_type=MESH)
     read_norm(0)
-    read_rope()
     nsq[...] = jnp.zeros_like(nsq)
     esq[...] = jnp.zeros_like(esq)
     hsq[...] = jnp.zeros_like(hsq)
@@ -489,7 +482,7 @@
             attend()
         elif name == "early":
             pl.semaphore_wait(barrier, 2 + len(partners))
-            early_begin()
+            start_all(early)
         elif name == "mean":
             first_means()
         elif name == "begin":
@@ -497,11 +490,11 @@
             begin(k)
             if k == 0:
                 start_all(hid_copies)
-                read_norm(1)
         elif name == "mid":
             middle(UNITS.index((arg, no)))
         elif name == "fin":
             if (arg, no) == UNITS[0]:
+                read_norm(1)
                 for copy in hid_copies:
                     copy.wait()
             finish(UNITS.index((arg, no)))
@@ -590,8 +583,8 @@
                 pltpu.SemaphoreType.DMA((NSLOT,)),
                 pltpu.SemaphoreType.DMA((n_units, 2, 3)),
                 pltpu.SemaphoreType.DMA((n_units, 2, 3)),
-                pltpu.SemaphoreType.DMA((2, 2)),
-                pltpu.SemaphoreType.DMA((2, 2)),
+                pltpu.SemaphoreType.DMA((2,)),
+                pltpu.SemaphoreType.DMA((2,)),
                 pltpu.SemaphoreType.DMA((6,)),
                 pltpu.SemaphoreType.DMA((n_tp,)),
                 pltpu.SemaphoreType.DMA,

time: 293 us -> 293 us (level)
  no operation moved by 1% of the time
where the time goes in v5:
time: 293 us
  Pallas kernels  292 us (100%)
    pallas_call x1, Pallas kernels, local_layer(): pl.pallas_call(functools.partial(layer_kernel, n_tp, n_dp), out_shape=(ja...  289 us

profile of v5, /device:TPU:1, one launch (start us, length us, event | category | flops | bytes accessed | tf_op | source)
XLA Modules:
  0.0 292.8 jit_solution(7229214095020189841)
XLA Ops:
  0.6 288.7 %layer.1 = (bf16[4,128,4096]{2,1,0:T(8,128)(2,1)}, f32[72,128]{1,0:T(8,128)}) custom-call(s32[1,128]{1,0:T(1,128)} %bitcast.12, f32[2,128]{1,0:T(2,128)} %constant.2.clone.freq_in, bf16[32,128]{1,0:T(8,128)(2,1)} %bitcast.8, bf16[32,128]{1,0:T(8,128)(2,1)} %bitcast.9, bf16[32,128]{1,0:T(8,128)(2,1)} %bitcast.10, bf16[32,128]{1,0:T(8,128)(2,1)} %bitcast.11, ...), custom_call_target="tpu_custom_call" | custom-call | tf_op jit(solution)/shard_map/layer/pallas_call | solution.py:552
  289.3 3.4 %final.1 = (bf16[4,128,4096]{2,1,0:T(8,128)(2,1)}, f32[32,128]{1,0:T(8,128)}, f32[32,128]{1,0:T(8,128)}, f32[1,12]{1,0:T(1,128)}) custom-call(bf16[4,128,4096]{2,1,0:T(8,128)(2,1)} %get-tuple-element.10.y_ref, f32[72,128]{1,0:T(8,128)} %get-tuple-element.11.score_ref), custom_call_target="tpu_custom_call" | custom-call | tf_op jit(solution)/shard_map/final/pallas_call | solution.py:602
